TPU v7x, 128 devices: a whole 4x4x4 slice. The times are simulated.
128 devices in a mesh: dp: 64 (over z_hi, x, y, core), mp: 2 (over z_lo).
Axes of the slice: x: 4, y: 4, z: 4 (z_hi: 2, z_lo: 2; z = z_hi * 2 + z_lo), core: 2. Of those that a mesh axis runs over, the one named last changes fastest.
Arguments:
- clean: float32 [256, 3, 4096], P(('dp', 'mp')), may hold values from -1 to 1
- noise: float32 [256, 3, 4096], P(('dp', 'mp')), may hold values from -12 to 12
- lowres: float32 [256, 3, 4096], P(('dp', 'mp')), may hold values from -1 to 1
- aug_noise: float32 [256, 3, 4096], P(('dp', 'mp')), may hold values from -5 to 5
- timesteps: int32 [256], P(('dp', 'mp')), may hold values from 0 to 999
- aug_levels: int32 [256], P(('dp', 'mp')), may hold values from 0 to 999
- lengths: int32 [256], P(('dp', 'mp')), may hold values from 1 to 128
- text: bfloat16 [256, 128, 4096], P(('dp', 'mp')), may hold values from -160 to 160
- w_stem: float32 [6, 128], replicated, may hold values from -2.5 to 2.5
- w_time: float32 [256, 256], replicated, may hold values from -0.375 to 0.375
- conv_one: bfloat16 [1152, 128], replicated, may hold values from -0.1875 to 0.1875
- conv_two: bfloat16 [1152, 128], replicated, may hold values from -0.1875 to 0.1875
- kv_weight: bfloat16 [4096, 256], P('mp'), may hold values from -0.09375 to 0.09375
- w_query: bfloat16 [128, 128], replicated, may hold values from -0.5 to 0.5
- w_output: bfloat16 [128, 128], replicated, may hold values from -0.5 to 0.5
- w_head: bfloat16 [3, 128], replicated, may hold values from -0.5 to 0.5
Outputs:
- conv_one_update: float32 [1152, 128], P(('dp', 'mp'))
- conv_two_update: float32 [1152, 128], P(('dp', 'mp'))
- kv_update: float32 [4096, 256], P('mp', 'dp')
- loss_mean: float32 [], replicated
All inputs are finite; a program needn't handle non-finite values.
Results may differ from a plain program's by a relative error of at most 0.03.
The roundings to bfloat16 on the way count: a program that leaves them out, or rounds other values in their place, can miss the bound.
Values may be sent and summed in bfloat16 or wider, within the bound.
A program may use at most 128 MiB of HBM per device.

v0:
```python
import functools
import math

import jax
import jax.numpy as jnp
from jax import lax
from jax.sharding import Mesh
from jax.sharding import PartitionSpec as P

S = 64
GROUPS = 32
HEADS = 2
HEAD_DIM = 64
FREQS = 64
STEPS = 1000
DP_MP = ("dp_0", "dp_1", "dp_2", "dp_3", "mp")
DP = ("dp_0", "dp_1", "dp_2", "dp_3")


def in_order(tiles, dim):
    tiles = jnp.moveaxis(tiles, 0, dim)
    dims = tiles.shape
    return tiles.reshape(*dims[:dim], dims[dim] * dims[dim + 1], *dims[dim + 2 :])


def from_everyone(array, axis):
    copies = jnp.broadcast_to(array, (lax.axis_size(axis), *array.shape))
    return lax.all_to_all(copies, axis, split_axis=0, concat_axis=0, tiled=True)


def gather_directly(array, axis, dim):
    return in_order(from_everyone(array, axis), dim)


def split_up(array, dim, count):
    dims = array.shape
    tiles = array.reshape(*dims[:dim], count, dims[dim] // count, *dims[dim + 1 :])
    return jnp.moveaxis(tiles, dim, 0)


def sum_together(arrays, axis, dims):
    count = lax.axis_size(axis)
    tiles = [split_up(a, dim, count) for a, dim in zip(arrays, dims)]
    lines = jnp.concatenate([b.reshape(count, -1) for b in tiles], axis=1)
    width = max(16, -(-lines.shape[1] // 1024) * 8)
    lines = jnp.pad(lines, ((0, 0), (0, width * 128 - lines.shape[1]))).reshape(-1, 128)
    line, at, finished = (lax.psum_scatter(lines, axis, tiled=True).reshape(-1), 0, [])
    for b in tiles:
        part = b[0]
        finished.append(line[at : at + part.size].reshape(part.shape))
        at += part.size
    return tuple(finished)


def sent_and_summed(array, axis, dim):
    tiles = split_up(array, dim, lax.axis_size(axis))
    arrived = lax.all_to_all(tiles, axis, split_axis=0, concat_axis=0, tiled=True)
    return arrived.sum(axis=0)


def over_axes(array, axes):
    return functools.reduce(lax.psum, axes, array)


def signal_level(index):
    ratio = (index.astype(jnp.float32) / STEPS + 0.008) / 1.008
    cosine = jnp.cos(ratio * (math.pi / 2.0))
    return cosine * cosine


def sinusoid(index):
    freqs = jnp.exp(-math.log(10000.0) * jnp.arange(FREQS, dtype=jnp.float32) / FREQS)
    angles = index.astype(jnp.float32) * freqs
    return jnp.concatenate([jnp.sin(angles), jnp.cos(angles)])


def prepare(clean, noise, lowres, aug_noise, tstep, level, w_stem, w_time):
    signal = signal_level(tstep)
    aug_signal = signal_level(level)
    noisy = jnp.sqrt(signal) * clean + jnp.sqrt(1.0 - signal) * noise
    low_noisy = jnp.sqrt(aug_signal) * lowres + jnp.sqrt(1.0 - aug_signal) * aug_noise
    stacked = jnp.concatenate([noisy, low_noisy], axis=0)
    h_start = jnp.einsum("kp,kc->pc", stacked, w_stem, precision=lax.Precision.HIGHEST)
    feature = jnp.concatenate([sinusoid(tstep), sinusoid(level)])[None, :]
    embed = jax.nn.silu(jnp.dot(feature, w_time, precision=lax.Precision.HIGHEST))[0]
    channels = w_stem.shape[1]
    return (h_start, embed[:channels], embed[channels:])


def group_matrix(channels):
    members = channels // GROUPS
    labels = jnp.arange(channels) // members
    return (labels[:, None] == labels[None, :]).astype(jnp.float32) / members


def group_norm(values, grouping):
    average = jnp.dot(
        jnp.mean(values, axis=0, keepdims=True), grouping, precision=lax.Precision.HIGHEST
    )
    centred = values - average
    spread = jnp.dot(
        jnp.mean(centred * centred, axis=0, keepdims=True),
        grouping,
        precision=lax.Precision.HIGHEST,
    )
    return centred * lax.rsqrt(spread + 1e-05)


def convolve(activation, weight):
    channels = weight.shape[1]
    kernel = weight.reshape(3, 3, channels, channels)
    picture = activation.reshape(1, S, S, channels)
    result = lax.conv_general_dilated(
        picture,
        kernel,
        (1, 1),
        "SAME",
        dimension_numbers=("NHWC", "HWIO", "NHWC"),
        preferred_element_type=jnp.float32,
    )
    return result.reshape(S * S, channels)


def image_loss(
    conv_one, conv_two, keys_values, h_start, scale, shift, keep, w_query, w_output, w_head, noise
):
    channels = conv_one.shape[1]
    grouping = group_matrix(channels)
    act_one = jax.nn.silu(group_norm(h_start, grouping)).astype(jnp.bfloat16)
    conv_out_one = convolve(act_one, conv_one)
    act_two = jax.nn.silu(group_norm(conv_out_one, grouping) * (1.0 + scale) + shift).astype(
        jnp.bfloat16
    )
    h_mid = h_start + convolve(act_two, conv_two)
    normed = group_norm(h_mid, grouping).astype(jnp.bfloat16)
    queries = (
        jnp.dot(normed, w_query, preferred_element_type=jnp.float32) * HEAD_DIM ** (-0.5)
    ).astype(jnp.bfloat16)
    width = w_query.shape[1]
    pieces = []
    for head_index in range(HEADS):
        lower = head_index * HEAD_DIM
        upper = lower + HEAD_DIM
        scores = jnp.dot(
            queries[:, lower:upper],
            keys_values[:, lower:upper].T,
            preferred_element_type=jnp.float32,
        )
        scores = jnp.where(keep[None, :], scores, -1e30)
        highest = jnp.max(scores, axis=1, keepdims=True)
        weights = jnp.exp(scores - highest)
        probs = (weights / jnp.sum(weights, axis=1, keepdims=True)).astype(jnp.bfloat16)
        pieces.append(
            jnp.dot(
                probs,
                keys_values[:, width + lower : width + upper],
                preferred_element_type=jnp.float32,
            )
        )
    attended = jnp.concatenate(pieces, axis=1).astype(jnp.bfloat16)
    h_out = h_mid + jnp.dot(attended, w_output, preferred_element_type=jnp.float32)
    pred = jnp.einsum(
        "kc,pc->kp", w_head, h_out.astype(jnp.bfloat16), preferred_element_type=jnp.float32
    )
    error = pred - noise
    return jnp.sum(error * error)


def local(
    clean,
    noise,
    lowres,
    aug_noise,
    timesteps,
    aug_levels,
    lengths,
    text,
    w_stem,
    w_time,
    conv_one,
    conv_two,
    kv_weight,
    w_query,
    w_output,
    w_head,
):
    images = clean.shape[0]
    tokens = text.shape[1]
    features = text.shape[2]
    width = kv_weight.shape[1]
    half = kv_weight.shape[0]
    piece = gather_directly(kv_weight, "mp", 0)
    flat = jnp.dot(
        text.reshape(images * tokens, piece.shape[0]), piece, preferred_element_type=jnp.float32
    )
    summed = flat.reshape(images, tokens, width)
    keys_values = summed.astype(jnp.bfloat16)

    def one_image(items):
        clean_i, noise_i, low_i, aug_i, tstep, level, length, pairs = items
        h_start, scale, shift = prepare(
            clean_i, noise_i, low_i, aug_i, tstep, level, w_stem, w_time
        )
        keep = jnp.arange(tokens) < length
        value, pullback = jax.vjp(
            lambda first, second, third: image_loss(
                first,
                second,
                third,
                h_start,
                scale,
                shift,
                keep,
                w_query,
                w_output,
                w_head,
                noise_i,
            ),
            conv_one,
            conv_two,
            pairs,
        )
        part_one, part_two, part_kv = pullback(jnp.ones((), jnp.float32))
        return (part_one, part_two, part_kv, value)

    parts_one, parts_two, parts_kv, values = lax.map(
        one_image, (clean, noise, lowres, aug_noise, timesteps, aug_levels, lengths, keys_values)
    )
    local_one = jnp.sum(parts_one.astype(jnp.float32), axis=0)
    local_two = jnp.sum(parts_two.astype(jnp.float32), axis=0)
    local_loss = jnp.sum(values)
    grad_one, grad_two = sum_together((local_one, local_two), DP_MP, (0, 0))
    full_grad = lax.dot_general(
        text.reshape(-1, features),
        parts_kv.reshape(-1, width),
        (((0,), (0,)), ((), ())),
        preferred_element_type=jnp.float32,
    )
    row_share = sent_and_summed(full_grad, "mp", 0)
    grad_kv = sent_and_summed(row_share, DP, 1)
    square_one = jnp.sum(grad_one * grad_one)
    square_two = jnp.sum(grad_two * grad_two)
    square_kv = jnp.sum(grad_kv * grad_kv)
    total_one, total_two, total_kv, loss_total = (
        over_axes(square_one, DP_MP),
        over_axes(square_two, DP_MP),
        over_axes(square_kv, DP_MP),
        over_axes(local_loss, DP_MP),
    )
    conv_count = conv_one.shape[0] * conv_one.shape[1]
    kv_count = half * lax.axis_size("mp") * width
    conv_one_update = grad_one * lax.rsqrt(total_one / conv_count + 1e-06)
    conv_two_update = grad_two * lax.rsqrt(total_two / conv_count + 1e-06)
    kv_update = grad_kv * lax.rsqrt(total_kv / kv_count + 1e-06)
    loss_mean = loss_total / (images * lax.axis_size(DP_MP) * clean.shape[1] * clean.shape[2])
    return (conv_one_update, conv_two_update, kv_update, loss_mean)


def solution(mesh):
    finer = Mesh(
        mesh.devices.reshape(2, 4, 4, 2, mesh.shape["mp"]), ("dp_0", "dp_1", "dp_2", "dp_3", "mp")
    )
    placed = (
        P(DP_MP, None, None),
        P(DP_MP, None, None),
        P(DP_MP, None, None),
        P(DP_MP, None, None),
        P(DP_MP),
        P(DP_MP),
        P(DP_MP),
        P(DP_MP, None, None),
        P(),
        P(),
        P(),
        P(),
        P("mp", None),
        P(),
        P(),
        P(),
    )
    return jax.shard_map(
        local,
        mesh=finer,
        in_specs=placed,
        out_specs=(P(DP_MP, None), P(DP_MP, None), P("mp", DP), P()),
        check_vma=False,
    )
```

profile of v0, /device:TPU:0, one launch (start us, length us, event | category | flops | bytes accessed | tf_op | source)
XLA Modules:
  0.0 514.2 jit_solution(8734797626247341750)
XLA Ops:
  7.2 2.8 broadcast_in_dim.132
  10.0 4.8 all-to-all-start
  14.8 25.5 %all-to-all-done = bf16[2,2048,256]{2,1,0:T(8,128)(2,1)} async-done(((bf16[2,2048,256]{2,1,0:T(8,128)(2,1)}), bf16[2,2048,256]{2,1,0:T(8,128)(2,1)}, u32[]{:S(2)}, u32[]{:S(2)}) %all-to-all-start) | async-done | bytes 2097184 | tf_op jit(solution)/shard_map/all_to_all | solution.py:28
  40.4 3.0 convolution_convert_fusion.11
  43.4 180.6 %while.19 = (s32[]{:T(128)}, bf16[2,1152,128]{2,1,0:T(8,128)(2,1)}, bf16[2,1152,128]{2,1,0:T(8,128)(2,1)}, bf16[2,128,256]{1,2,0:T(8,128)(2,1)}, f32[2]{0:T(128)...) while((s32[]{:T(128)}, bf16[2,1152,128]{2,1,0:T(8,128)(2,1)}, ...), condition=%wide.region_22.23_spmd, body=%wide.region_0.22_spmd.sunk | while | flops 8245876736 | bytes 325935872 | solution.py:226
  43.7 1.2 dynamic_slice.78
  51.1 3.5 fusion.458
  58.1 3.0 select_reduce_fusion.8
  63.5 1.5 fusion.468
  66.0 3.1 fusion.470
  75.8 2.1 convert_reduce_fusion.7
  80.0 2.1 convert_reduce_fusion.6
  84.3 4.0 multiply_reduce_fusion.17
  88.3 1.5 convolution_convert_fusion.22
  89.8 1.4 convolution_convert_fusion.23
  100.0 1.5 multiply_reduce_fusion.20
  106.1 4.2 select_reduce_fusion.10
  114.6 4.3 fusion.493
  121.4 5.0 fusion.486
  139.3 3.5 fusion.458
  146.4 3.0 select_reduce_fusion.8
  153.9 3.1 fusion.470
  163.8 2.1 convert_reduce_fusion.7
  167.9 2.1 convert_reduce_fusion.6
  172.2 4.0 multiply_reduce_fusion.17
  176.2 1.5 convolution_convert_fusion.22
  177.7 1.6 convolution_convert_fusion.23
  188.2 1.5 multiply_reduce_fusion.20
  194.3 4.1 select_reduce_fusion.10
  202.8 4.3 fusion.493
  209.6 4.8 fusion.486
  224.0 1.6 fusion.298
  226.1 50.8 %all_to_all.15 = f32[2,2048,256]{1,2,0:T(8,128)} all-to-all(f32[2,2048,256]{1,2,0:T(8,128)S(1)} %bitcast.338), channel_id=1, replica_groups=mesh['dp_0'=2,'dp_1'=4,'dp_2'=4,'dp_3'=2,'mp'=2] {'mp'}, dimensions={0} | all-to-all | bytes 8388608 | tf_op jit(solution)/shard_map/all_to_all | solution.py:57
  276.9 4.0 reduce_sum.355
  280.9 2.9 reshape.369
  283.8 11.0 %all-to-all-start.2 = ((f32[64,2048,4]{1,2,0:T(4,128)}), f32[64,2048,4]{1,2,0:T(4,128)}, u32[]{:S(2)}, u32[]{:S(2)}) async-start(f32[64,2048,4]{1,2,0:T(4,128)} %bitcast.339), calls=%async_computation.2 | async-start | bytes 4194304 | tf_op jit(solution)/shard_map/all_to_all | solution.py:57
  294.8 1.5 convert_reduce_fusion.2
  297.4 2.4 select_maximum_fusion.1
  299.8 2.6 reshape.367
  303.1 157.6 %all-reduce.15.cloned.1.call-done = f32[3072,128]{1,0:T(8,128)} async-done(((f32[3072,128]{1,0:T(8,128)}), f32[3072,128]{1,0:T(8,128)}) %all-reduce.15.cloned.1.call-update) | async-done | bytes 1572880
  460.6 1.4 multiply_reduce_fusion.7
  462.0 1.9 reduce_sum.356
  464.6 7.1 %all-reduce.12 = (f32[]{:T(128)}, f32[]{:T(128)}, f32[]{:T(128)}, f32[]{:T(128)}) all-reduce(f32[]{:T(128)} %get-tuple-element.372, f32[]{:T(128)} %get-tuple-element.371, f32[]{:T(128)} %multiply_reduce_fusion.6, f32[]{:T(128)} %reduce_sum.358), channel_id=1, replica_groups=mesh['dp_0'=2,'dp_1'=4,'dp_2'=4,'dp_3'=2,'mp'=2] {'dp_0'}, use_global_device_ids=true, to_apply=%region_27.28 | all-reduce | flops 4 | bytes 32 | tf_op jit(solution)/shard_map/psum | solution.py:62
  471.6 9.9 %all-reduce.9 = (f32[]{:T(128)}, f32[]{:T(128)}, f32[]{:T(128)}, f32[]{:T(128)}) all-reduce(f32[]{:T(128)} %get-tuple-element.429, f32[]{:T(128)} %get-tuple-element.430, f32[]{:T(128)} %get-tuple-element.431, f32[]{:T(128)} %get-tuple-element.432), channel_id=1, replica_groups=mesh['dp_0'=2,'dp_1'=4,'dp_2'=4,'dp_3'=2,'mp'=2] {'dp_1'}, use_global_device_ids=true, to_apply=%region_28.29 | all-reduce | flops 4 | bytes 32 | tf_op jit(solution)/shard_map/psum | solution.py:62
  481.5 11.1 %all-reduce.8 = (f32[]{:T(128)}, f32[]{:T(128)}, f32[]{:T(128)}, f32[]{:T(128)}) all-reduce(f32[]{:T(128)} %get-tuple-element.417, f32[]{:T(128)} %get-tuple-element.418, f32[]{:T(128)} %get-tuple-element.419, f32[]{:T(128)} %get-tuple-element.420), channel_id=1, replica_groups=mesh['dp_0'=2,'dp_1'=4,'dp_2'=4,'dp_3'=2,'mp'=2] {'dp_2'}, use_global_device_ids=true, to_apply=%region_29.30 | all-reduce | flops 4 | bytes 32 | tf_op jit(solution)/shard_map/psum | solution.py:62
  492.6 3.1 all-reduce.11
  495.7 5.6 %all-reduce.10 = (f32[]{:T(128)}, f32[]{:T(128)}, f32[]{:T(128)}, f32[]{:T(128)}) all-reduce(f32[]{:T(128)} %get-tuple-element.425, f32[]{:T(128)} %get-tuple-element.426, f32[]{:T(128)} %get-tuple-element.427, f32[]{:T(128)} %get-tuple-element.428), channel_id=1, replica_groups=mesh['dp_0'=2,'dp_1'=4,'dp_2'=4,'dp_3'=2,'mp'=2] {'mp'}, use_global_device_ids=true, to_apply=%region_31.32 | all-reduce | flops 4 | bytes 32 | tf_op jit(solution)/shard_map/psum | solution.py:62
  504.5 1.4 dynamic-slice_multiply_fusion
  (461 shorter events, 92.1 us)
Async XLA Ops:
  7.2 33.2 %copy-start = (bf16[2,128,4096]{2,1,0:T(8,128)(2,1)S(1)}, bf16[2,128,4096]{2,1,0:T(8,128)(2,1)}, u32[]{:S(2)}) copy-start(bf16[2,128,4096]{2,1,0:T(8,128)(2,1)} %param.25) | copy-start | bytes 6291460
  10.0 30.3 %all-to-all-start = ((bf16[2,2048,256]{2,1,0:T(8,128)(2,1)}), bf16[2,2048,256]{2,1,0:T(8,128)(2,1)}, u32[]{:S(2)}, u32[]{:S(2)}) async-start(bf16[2,2048,256]{2,1,0:T(8,128)(2,1)} %broadcast_in_dim.132), calls=%async_computation | async-start | bytes 4194304 | tf_op jit(solution)/shard_map/all_to_all | solution.py:28
  40.3 3.0 copy-start.26
  40.3 3.0 copy-start.30
  40.3 3.1 copy-start.54
  40.4 3.0 copy-start.59
  40.4 3.0 copy-start.61
  54.5 17.8 %copy-start.66 = (s32[128]{0:T(128)}, s32[128]{0:T(128)S(1)}, u32[]{:S(2)}) copy-start(s32[128]{0:T(128)S(1)} %and_select_fusion.2) | copy-start | bytes 1540 | tf_op jit(solution)/shard_map/while
  61.2 3.8 copy-start.7
  61.4 3.6 copy-start.40
  63.5 2.5 copy-start.57
  65.0 4.0 copy-start.9
  73.7 5.4 %copy-start.15 = (bf16[4096,128]{0,1:T(8,128)(2,1)}, bf16[4096,128]{0,1:T(8,128)(2,1)S(1)}, u32[]{:S(2)}) copy-start(bf16[4096,128]{0,1:T(8,128)(2,1)S(1)} %fusion.473) | copy-start | bytes 3145732 | tf_op jit(solution)/shard_map/while
  75.1 4.1 copy-start.42
  75.8 3.3 copy-start.21
  79.6 2.5 copy-start.5
  79.9 4.4 copy-start.23
  88.3 2.9 copy-start.24
  88.3 3.0 copy-start.6
  106.1 4.2 copy-start.68
  121.3 5.1 copy-start.34
  121.3 5.1 copy-start.36
  121.4 5.2 %copy-start.63 = (f32[2]{0:T(128)S(1)}, f32[2]{0:T(128)}, u32[]{:S(2)}) copy-start(f32[2]{0:T(128)} %get-tuple-element.739) | copy-start | bytes 28 | tf_op jit(solution)/shard_map/while
  121.4 6.5 %copy-start.27 = (bf16[128,128]{1,0:T(8,128)(2,1)S(1)}, bf16[128,128]{1,0:T(8,128)(2,1)}, u32[]{:S(2)}) copy-start(bf16[128,128]{1,0:T(8,128)(2,1)} %get-tuple-element.823) | copy-start | bytes 98308 | tf_op jit(solution)/shard_map/while
  121.4 6.5 %copy-start.55 = (f32[6,128]{1,0:T(8,128)S(1)}, f32[6,128]{1,0:T(8,128)}, u32[]{:S(2)}) copy-start(f32[6,128]{1,0:T(8,128)} %get-tuple-element.882) | copy-start | bytes 9220 | tf_op jit(solution)/shard_map/while
  121.4 6.5 %copy-start.60 = (s32[2]{0:T(128)S(1)}, s32[2]{0:T(128)}, u32[]{:S(2)}) copy-start(s32[2]{0:T(128)} %get-tuple-element.914) | copy-start | bytes 28 | tf_op jit(solution)/shard_map/while
  121.4 6.5 %copy-start.62 = (s32[2]{0:T(128)S(1)}, s32[2]{0:T(128)}, u32[]{:S(2)}) copy-start(s32[2]{0:T(128)} %get-tuple-element.946) | copy-start | bytes 28 | tf_op jit(solution)/shard_map/while
  142.8 17.5 %copy-start.66 = (s32[128]{0:T(128)}, s32[128]{0:T(128)S(1)}, u32[]{:S(2)}) copy-start(s32[128]{0:T(128)S(1)} %and_select_fusion.2) | copy-start | bytes 1540 | tf_op jit(solution)/shard_map/while
  149.4 3.5 copy-start.7
  149.6 3.3 copy-start.40
  153.0 4.0 copy-start.9
  161.7 5.4 %copy-start.15 = (bf16[4096,128]{0,1:T(8,128)(2,1)}, bf16[4096,128]{0,1:T(8,128)(2,1)S(1)}, u32[]{:S(2)}) copy-start(bf16[4096,128]{0,1:T(8,128)(2,1)S(1)} %fusion.473) | copy-start | bytes 3145732 | tf_op jit(solution)/shard_map/while
  163.0 4.1 copy-start.42
  163.8 3.3 copy-start.21
  167.9 4.4 copy-start.23
  176.2 3.2 copy-start.24
  176.2 3.2 copy-start.6
  194.3 4.2 copy-start.68
  209.5 4.9 copy-start.34
  209.5 4.9 copy-start.36
  209.5 5.0 copy-start.63
  209.5 6.3 %copy-start.27 = (bf16[128,128]{1,0:T(8,128)(2,1)S(1)}, bf16[128,128]{1,0:T(8,128)(2,1)}, u32[]{:S(2)}) copy-start(bf16[128,128]{1,0:T(8,128)(2,1)} %get-tuple-element.823) | copy-start | bytes 98308 | tf_op jit(solution)/shard_map/while
  209.5 6.3 %copy-start.55 = (f32[6,128]{1,0:T(8,128)S(1)}, f32[6,128]{1,0:T(8,128)}, u32[]{:S(2)}) copy-start(f32[6,128]{1,0:T(8,128)} %get-tuple-element.882) | copy-start | bytes 9220 | tf_op jit(solution)/shard_map/while
  209.5 6.3 %copy-start.60 = (s32[2]{0:T(128)S(1)}, s32[2]{0:T(128)}, u32[]{:S(2)}) copy-start(s32[2]{0:T(128)} %get-tuple-element.914) | copy-start | bytes 28 | tf_op jit(solution)/shard_map/while
  209.6 6.3 %copy-start.62 = (s32[2]{0:T(128)S(1)}, s32[2]{0:T(128)}, u32[]{:S(2)}) copy-start(s32[2]{0:T(128)} %get-tuple-element.946) | copy-start | bytes 28 | tf_op jit(solution)/shard_map/while
  283.8 178.3 %all-to-all-start.2 = ((f32[64,2048,4]{1,2,0:T(4,128)}), f32[64,2048,4]{1,2,0:T(4,128)}, u32[]{:S(2)}, u32[]{:S(2)}) async-start(f32[64,2048,4]{1,2,0:T(4,128)} %bitcast.339), calls=%async_computation.2 | async-start | bytes 4194304 | tf_op jit(solution)/shard_map/all_to_all | solution.py:57
  294.8 165.8 %all-reduce.15.cloned.1.call-start = ((), (), s32[]{:S(2)}) async-start(), calls=%async_computation.3 | async-start | bytes 3145728
  299.8 2.6 copy-start.65
  (88 other events, 122.3 us)
Sparse Core Ops, SparseCore 0:
  302.6 158.0 all-reduce.14
where the time goes:
time: 518 us; the launch traced here: 514 us
  waiting for transfers between devices  183 us (35%)
  matrix products  91.3 us (18%)
  blocking collectives  87.4 us (17%)
  local copies, waits for them, and re-layouts  56.2 us (11%)
  other arithmetic  44.4 us (9%)
  between operations  18.2 us (4%)
  loops' own time  17.7 us (3%)
  starting transfers between devices  15.9 us (3%)
    unnamed x2, waiting for transfers between devices  158 us
    all_to_all x1, blocking collectives, sent_and_summed(): lax.all_to_all(tiles, axis, split_axis=0, concat_axis=0, tiled=True)  50.8 us
    conv_general_dilated x10, matrix products, convolve(): lax.conv_general_dilated(picture, kernel, (1, 1), 'SAME', dimension_numbe...  39.1 us
    psum x5, blocking collectives, over_axes(): return functools.reduce(lax.psum, axes, array)  36.7 us
    all_to_all x1, waiting for transfers between devices, from_everyone(): return lax.all_to_all(copies, axis, split_axis=0, concat_axis=0, tiled=True)  25.5 us
    another operation x1, loops' own time, local(): lax.map(one_image, (clean, noise, lowres, aug_noise, timesteps, aug_level...  17.7 us
    while x260, local copies, waits for them, and re-layouts  17.2 us
    dynamic_slice x14, local copies, waits for them, and re-layouts, local(): lax.map(one_image, (clean, noise, lowres, aug_noise, timesteps, aug_level...  12.6 us
  transfers between devices with their start and end apart: 3, of which 2 were waited for; matrix products, arithmetic and copies ran while one was open for 2% of the time, Pallas kernels for 0%

commit v1 on v0

--- a/solution.py
+++ b/solution.py
@@ -6,6 +6,8 @@
 from jax import lax
 from jax.sharding import Mesh
 from jax.sharding import PartitionSpec as P
+from jax.experimental import pallas as pl
+from jax.experimental.pallas import tpu as pltpu
 
 S = 64
 GROUPS = 32
@@ -166,6 +168,305 @@
     return jnp.sum(error * error)
 
 
+AXES = ("dp_0", "dp_1", "dp_2", "dp_3", "mp")
+MESH = pl.DeviceIdType.MESH
+LINE = 4
+
+
+def axis_target(axis, to):
+    if axis == "x":
+        return {"dp_1": to}
+    if axis == "y":
+        return {"dp_2": to}
+    if axis == "z":
+        return {"dp_0": to // 2, "mp": lax.rem(to, 2)}
+    return {"dp_3": to}
+
+
+ORDERS = (("x", "y", "z"), ("y", "z", "x"), ("z", "x", "y"))
+DIMS = {0: ("x", "y", "z"), 1: None}
+
+
+def part_of(ref, left, axis, at):
+    index = tuple(at if name == axis else slice(None) for name in left)
+    return ref.at[index]
+
+
+def finish_kernel(
+    counts,
+    text_ref,
+    cot_ref,
+    conv_ref,
+    loss_ref,
+    one_ref,
+    two_ref,
+    kv_ref,
+    mean_ref,
+    rows_ref,
+    wide_ref,
+    own_a,
+    own_b,
+    core_in,
+    held,
+    line_in,
+    second,
+    second_in,
+    third,
+    third_in,
+    total_ref,
+    slots,
+    send_sems,
+    recv_sems,
+    slot_send,
+    slot_recv,
+):
+    place = {
+        "x": lax.axis_index("dp_1"),
+        "y": lax.axis_index("dp_2"),
+        "z": lax.axis_index("dp_0") * 2 + lax.axis_index("mp"),
+        "core": lax.axis_index("dp_3"),
+    }
+    core = place["core"]
+    other = 1 - core
+    barrier = pltpu.get_barrier_semaphore()
+    pl.semaphore_signal(
+        barrier, inc=1, device_id=axis_target("core", other), device_id_type=MESH
+    )
+    for axis in ("x", "y", "z"):
+        for k in range(1, LINE):
+            to = lax.rem(place[axis] + k, LINE)
+            pl.semaphore_signal(
+                barrier, inc=1, device_id=axis_target(axis, to), device_id_type=MESH
+            )
+
+    tokens = cot_ref.shape[0]
+    for q in range(4):
+        row = lax.broadcasted_iota(jnp.int32, (1024, 256), 0)
+        col = lax.broadcasted_iota(jnp.int32, (1024, 256), 1)
+        j = row % 4
+        qq = (row // 4) % 4
+        zh = (row // 16) % 2
+        y = (row // 32) % 4
+        x = (row // 128) % 4
+        c = row // 512
+        source = (((zh * 4 + x) * 4 + y) * 2 + c) * 4 + j
+        pick = jnp.where((source == col) & (qq == q), 1.0, 0.0).astype(jnp.bfloat16)
+        rows_ref[:, q * tokens : (q + 1) * tokens] = lax.dot_general(
+            pick,
+            cot_ref[...],
+            (((1,), (1,)), ((), ())),
+            preferred_element_type=jnp.float32,
+        ).astype(jnp.bfloat16)
+        for m in range(2):
+            wide_ref[q * tokens : (q + 1) * tokens, m * 512 : (m + 1) * 512] = text_ref[
+                :, m * 2048 + q * 512 : m * 2048 + (q + 1) * 512
+            ]
+
+    def block(i, carry):
+        rows = rows_ref[pl.ds(pl.multiple_of(i * 128, 128), 128), :]
+        for m in range(2):
+            value = jnp.dot(
+                rows, wide_ref[:, m * 512 : (m + 1) * 512], preferred_element_type=jnp.float32
+            ).astype(jnp.bfloat16)
+            value = value.reshape(4, 2, 16, 512)
+            at = lax.rem(i, 4)
+            for zh in range(2):
+                own_a[i // 4, at, :, zh * 2 + m] = value[:, zh, :, :256]
+                own_b[i // 4, at, :, zh * 2 + m] = value[:, zh, :, 256:]
+        return carry
+
+    lax.fori_loop(0, 8, block, 0)
+
+    pl.semaphore_wait(barrier, 10)
+
+    firsts = (own_a, own_b, conv_ref)
+    copies = []
+    for c in range(3):
+        copy = pltpu.make_async_remote_copy(
+            src_ref=firsts[c].at[other],
+            dst_ref=core_in.at[c],
+            send_sem=send_sems.at[c],
+            recv_sem=recv_sems.at[c],
+            device_id=axis_target("core", other),
+            device_id_type=MESH,
+        )
+        copy.start()
+        copies.append(copy)
+
+    def exchange(c, stage, source, left, into):
+        axis = ORDERS[c][stage]
+        started = []
+        for k in range(1, LINE):
+            to = lax.rem(place[axis] + k, LINE)
+            slot = 3 + (c * 3 + stage) * 3 + k - 1
+            copy = pltpu.make_async_remote_copy(
+                src_ref=part_of(source.at[c], left, axis, to),
+                dst_ref=into.at[c, k - 1],
+                send_sem=send_sems.at[slot],
+                recv_sem=recv_sems.at[slot],
+                device_id=axis_target(axis, to),
+                device_id_type=MESH,
+            )
+            copy.start()
+            started.append(copy)
+        return started
+
+    lines = []
+    for c in range(3):
+        copies[c].wait_recv()
+
+        def add(i, carry, c=c):
+            held[c, i] = (
+                firsts[c][core, i].astype(jnp.float32) + core_in[c, i].astype(jnp.float32)
+            ).astype(jnp.bfloat16)
+            return carry
+
+        lax.fori_loop(0, LINE, add, 0)
+        lines.append(exchange(c, 0, held, ("x", "y", "z"), line_in))
+
+    def own_part(ref, c, left, axis):
+        index = tuple(place[axis] if name == axis else slice(None) for name in left)
+        return ref[(c,) + index]
+
+    seconds = []
+    for c in range(3):
+        axis = ORDERS[c][0]
+        for copy in lines[c]:
+            copy.wait_recv()
+        for i in range(LINE):
+            rest = [name for name in ("x", "y", "z") if name != axis]
+            index = tuple(
+                place[axis] if name == axis else (i if name == rest[0] else slice(None))
+                for name in ("x", "y", "z")
+            )
+            value = held[(c,) + index].astype(jnp.float32)
+            for k in range(LINE - 1):
+                value = value + line_in[c, k, i].astype(jnp.float32)
+            second[c, i] = value.astype(jnp.bfloat16)
+        left = tuple(name for name in ("x", "y", "z") if name != axis)
+        seconds.append(exchange(c, 1, second, left, second_in))
+
+    thirds = []
+    for c in range(3):
+        left = tuple(name for name in ("x", "y", "z") if name != ORDERS[c][0])
+        axis = ORDERS[c][1]
+        for copy in seconds[c]:
+            copy.wait_recv()
+        value = own_part(second, c, left, axis).astype(jnp.float32)
+        for k in range(LINE - 1):
+            value = value + second_in[c, k].astype(jnp.float32)
+        third[c] = value.astype(jnp.bfloat16)
+        thirds.append(exchange(c, 2, third, (ORDERS[c][2],), third_in))
+
+    for c in range(3):
+        axis = ORDERS[c][2]
+        for copy in thirds[c]:
+            copy.wait_recv()
+        value = third[c, place[axis]].astype(jnp.float32)
+        for k in range(LINE - 1):
+            value = value + third_in[c, k].astype(jnp.float32)
+        total_ref[:, c * 256 : (c + 1) * 256] = value
+
+    value = total_ref[...]
+    square = value * value
+    kv_line = jnp.sum(square[:, :512], axis=0, keepdims=True)
+    kv_line = (
+        kv_line[:, :128] + kv_line[:, 128:256] + kv_line[:, 256:384] + kv_line[:, 384:512]
+    )
+    conv_line = jnp.sum(square[:, 512:], axis=0, keepdims=True)
+    row = lax.broadcasted_iota(jnp.int32, (8, 128), 0)
+    tile = jnp.where(row == 0, kv_line, 0.0)
+    tile = jnp.where(row == 1, conv_line[:, :128], tile)
+    tile = jnp.where(row == 2, conv_line[:, 128:], tile)
+    tile = jnp.where(row == 3, loss_ref[...], tile)
+    at = 0
+    for stage, axis in enumerate(("core", "x", "y", "z")):
+        size = 2 if axis == "core" else LINE
+        slots[stage, place[axis]] = tile
+        started = []
+        for k in range(1, size):
+            to = lax.rem(place[axis] + k, size)
+            copy = pltpu.make_async_remote_copy(
+                src_ref=slots.at[stage, place[axis]],
+                dst_ref=slots.at[stage, place[axis]],
+                send_sem=slot_send.at[at],
+                recv_sem=slot_recv.at[at],
+                device_id=axis_target(axis, to),
+                device_id_type=MESH,
+            )
+            copy.start()
+            started.append(copy)
+            at += 1
+        for copy in started:
+            copy.wait_recv()
+        tile = slots[stage, 0]
+        for k in range(1, size):
+            tile = tile + slots[stage, k]
+        for copy in started:
+            copy.wait_send()
+    sums = jnp.sum(tile, axis=1, keepdims=True)
+    kv_scale = lax.rsqrt(sums[0:1] / counts[0] + 1e-06)
+    one_scale = lax.rsqrt(sums[1:2] / counts[1] + 1e-06)
+    two_scale = lax.rsqrt(sums[2:3] / counts[1] + 1e-06)
+    one_ref[...] = total_ref[0:9, 512:640] * one_scale
+    two_ref[...] = total_ref[0:9, 640:768] * two_scale
+    for q in range(4):
+        kv_ref[:, q * 512 : (q + 1) * 512] = total_ref[q * 4 : (q + 1) * 4, 0:512] * kv_scale
+    mean_ref[...] = jnp.broadcast_to(sums[3:4] / counts[2], mean_ref.shape)
+    for copy in copies:
+        copy.wait_send()
+    for group in lines + seconds + thirds:
+        for copy in group:
+            copy.wait_send()
+
+
+def finish(text, cot, conv, loss, counts):
+    bf16, f32 = jnp.bfloat16, jnp.float32
+    return pl.pallas_call(
+        functools.partial(finish_kernel, counts),
+        out_shape=(
+            jax.ShapeDtypeStruct((9, 128), f32),
+            jax.ShapeDtypeStruct((9, 128), f32),
+            jax.ShapeDtypeStruct((4, 2048), f32),
+            jax.ShapeDtypeStruct((1, 128), f32),
+        ),
+        in_specs=[pl.BlockSpec(memory_space=pltpu.VMEM)] * 4,
+        out_specs=[pl.BlockSpec(memory_space=pltpu.VMEM)] * 4,
+        scratch_shapes=[
+            pltpu.VMEM((1024, 1024), bf16),
+            pltpu.VMEM((1024, 1024), bf16),
+            pltpu.VMEM((2, 4, 4, 4, 16, 256), bf16),
+            pltpu.VMEM((2, 4, 4, 4, 16, 256), bf16),
+            pltpu.VMEM((3, 4, 4, 4, 16, 256), bf16),
+            pltpu.VMEM((3, 4, 4, 4, 16, 256), bf16),
+            pltpu.VMEM((3, 3, 4, 4, 16, 256), bf16),
+            pltpu.VMEM((3, 4, 4, 16, 256), bf16),
+            pltpu.VMEM((3, 3, 4, 16, 256), bf16),
+            pltpu.VMEM((3, 4, 16, 256), bf16),
+            pltpu.VMEM((3, 3, 16, 256), bf16),
+            pltpu.VMEM((16, 768), f32),
+            pltpu.VMEM((4, 4, 8, 128), f32),
+            pltpu.SemaphoreType.DMA((30,)),
+            pltpu.SemaphoreType.DMA((30,)),
+            pltpu.SemaphoreType.DMA((10,)),
+            pltpu.SemaphoreType.DMA((10,)),
+        ],
+        compiler_params=pltpu.CompilerParams(
+            collective_id=0, has_side_effects=True, vmem_limit_bytes=40 * 2**20
+        ),
+        cost_estimate=pl.CostEstimate(
+            flops=3 * 10**9, bytes_accessed=8 * 10**6, transcendentals=0
+        ),
+        name="finish",
+    )(text, cot, conv, loss)
+
+
+def by_owner(grad):
+    tiles = grad.reshape(2, 4, 4, 2, 2, 9, 128)
+    tiles = jnp.transpose(tiles, (3, 1, 2, 0, 4, 5, 6)).reshape(2, 4, 4, 4, 9, 128)
+    return jnp.pad(tiles, ((0, 0),) * 4 + ((0, 7), (0, 0))).astype(jnp.bfloat16)
+
+
 def local(
     clean,
     noise,
@@ -229,31 +530,18 @@
     local_one = jnp.sum(parts_one.astype(jnp.float32), axis=0)
     local_two = jnp.sum(parts_two.astype(jnp.float32), axis=0)
     local_loss = jnp.sum(values)
-    grad_one, grad_two = sum_together((local_one, local_two), DP_MP, (0, 0))
-    full_grad = lax.dot_general(
-        text.reshape(-1, features),
-        parts_kv.reshape(-1, width),
-        (((0,), (0,)), ((), ())),
-        preferred_element_type=jnp.float32,
-    )
-    row_share = sent_and_summed(full_grad, "mp", 0)
-    grad_kv = sent_and_summed(row_share, DP, 1)
-    square_one = jnp.sum(grad_one * grad_one)
-    square_two = jnp.sum(grad_two * grad_two)
-    square_kv = jnp.sum(grad_kv * grad_kv)
-    total_one, total_two, total_kv, loss_total = (
-        over_axes(square_one, DP_MP),
-        over_axes(square_two, DP_MP),
-        over_axes(square_kv, DP_MP),
-        over_axes(local_loss, DP_MP),
-    )
-    conv_count = conv_one.shape[0] * conv_one.shape[1]
-    kv_count = half * lax.axis_size("mp") * width
-    conv_one_update = grad_one * lax.rsqrt(total_one / conv_count + 1e-06)
-    conv_two_update = grad_two * lax.rsqrt(total_two / conv_count + 1e-06)
-    kv_update = grad_kv * lax.rsqrt(total_kv / kv_count + 1e-06)
-    loss_mean = loss_total / (images * lax.axis_size(DP_MP) * clean.shape[1] * clean.shape[2])
-    return (conv_one_update, conv_two_update, kv_update, loss_mean)
+    conv = jnp.concatenate([by_owner(local_one), by_owner(local_two)], axis=-1)
+    counts = (
+        2 * half * width,
+        conv_one.shape[0] * conv_one.shape[1],
+        images * lax.axis_size(DP_MP) * clean.shape[1] * clean.shape[2],
+    )
+    lane = lax.broadcasted_iota(jnp.int32, (1, 128), 1)
+    loss = jnp.where(lane == 0, local_loss, 0.0)
+    conv_one_update, conv_two_update, kv, mean = finish(
+        text.reshape(-1, features), parts_kv.reshape(-1, width), conv, loss, counts
+    )
+    return (conv_one_update, conv_two_update, kv.T, mean[0, 0])
 
 
 def solution(mesh):

time: 518 us -> 284 us (0.55)
  waiting for transfers between devices: 183 us -> 25.4 us
  blocking collectives: 87.4 us -> 0 us
  Pallas kernels: 0 us -> 38.3 us
  between operations: 18.2 us -> 2.28 us
  starting transfers between devices: 15.9 us -> 4.94 us
  other arithmetic: 44.4 us -> 36 us
  local copies, waits for them, and re-layouts: 56.2 us -> 63.9 us
    unnamed x2 -> x0, waiting for transfers between devices: 158 us -> none
    all_to_all x1 -> x0, blocking collectives: 50.8 us -> none  [sent_and_summed(): lax.all_to_all(tiles, axis, split_axis=0, concat_axis=0, tiled=True)]
    pallas_call x0 -> x1, Pallas kernels: none -> 38.3 us  [finish(): pl.pallas_call(functools.partial(finish_kernel, counts), out_shape=(jax.S...]
    psum x5 -> x0, blocking collectives: 36.7 us -> none  [over_axes(): return functools.reduce(lax.psum, axes, array)]
    all_to_all x1 -> x0, starting transfers between devices: 11 us -> none  [sent_and_summed(): lax.all_to_all(tiles, axis, split_axis=0, concat_axis=0, tiled=True)]
    reduce_sum x4 -> x1, other arithmetic: 7.95 us -> 1.29 us  [local(): local_one = jnp.sum(parts_one.astype(jnp.float32), axis=0)]
    dynamic_update_slice x4 -> x8, local copies, waits for them, and re-layouts: 1.68 us -> 8.15 us  [local(): lax.map(one_image, (clean, noise, lowres, aug_noise, timesteps, aug_level...]
    reshape x3 -> x2, local copies, waits for them, and re-layouts: 5.96 us -> 0.25 us  [by_owner(): tiles = grad.reshape(2, 4, 4, 2, 2, 9, 128)]
  transfers between devices with their start and end apart: 3 -> 1, of which waited for: 2 -> 1; matrix products, arithmetic and copies ran while one was open for 2% -> 0% of each run, Pallas kernels for 0% -> 0%
where the time goes in v1:
time: 284 us; the launch traced here: 281 us
  matrix products  94.6 us (33%)
  local copies, waits for them, and re-layouts  63.9 us (22%)
  Pallas kernels  38.3 us (13%)
  other arithmetic  36 us (13%)
  waiting for transfers between devices  25.4 us (9%)
  loops' own time  15.4 us (5%)
  starting transfers between devices  4.94 us (2%)
    conv_general_dilated x10, matrix products, convolve(): lax.conv_general_dilated(picture, kernel, (1, 1), 'SAME', dimension_numbe...  39 us
    pallas_call x1, Pallas kernels, finish(): pl.pallas_call(functools.partial(finish_kernel, counts), out_shape=(jax.S...  38.3 us
    all_to_all x1, waiting for transfers between devices, from_everyone(): return lax.all_to_all(copies, axis, split_axis=0, concat_axis=0, tiled=True)  25.4 us
    while x280, local copies, waits for them, and re-layouts  22.6 us
    another operation x1, loops' own time, local(): lax.map(one_image, (clean, noise, lowres, aug_noise, timesteps, aug_level...  15.4 us
    dynamic_slice x14, local copies, waits for them, and re-layouts, local(): lax.map(one_image, (clean, noise, lowres, aug_noise, timesteps, aug_level...  12.6 us
    dot_general x4, matrix products, image_loss(): jnp.einsum('kc,pc->kp', w_head, h_out.astype(jnp.bfloat16), preferred_ele...  12.4 us
    dot_general x12, matrix products, image_loss(): jnp.dot(probs, keys_values[:, width + lower:width + upper], preferred_ele...  10.3 us
  transfers between devices with their start and end apart: 1, of which 1 were waited for; matrix products, arithmetic and copies ran while one was open for 0% of the time, Pallas kernels for 0%

profile of v1, /device:TPU:0, one launch (start us, length us, event | category | flops | bytes accessed | tf_op | source)
XLA Modules:
  0.0 280.9 jit_solution(12048141244794891687)
XLA Ops:
  0.6 2.7 broadcast_in_dim.140
  3.3 4.9 %all-to-all-start = ((bf16[2,2048,256]{2,1,0:T(8,128)(2,1)}), bf16[2,2048,256]{2,1,0:T(8,128)(2,1)}, u32[]{:S(2)}, u32[]{:S(2)}) async-start(bf16[2,2048,256]{2,1,0:T(8,128)(2,1)} %broadcast_in_dim.140), calls=%async_computation | async-start | bytes 4194304 | tf_op jit(solution)/shard_map/all_to_all | solution.py:30
  8.3 25.4 %all-to-all-done = bf16[2,2048,256]{2,1,0:T(8,128)(2,1)} async-done(((bf16[2,2048,256]{2,1,0:T(8,128)(2,1)}), bf16[2,2048,256]{2,1,0:T(8,128)(2,1)}, u32[]{:S(2)}, u32[]{:S(2)}) %all-to-all-start) | async-done | bytes 2097184 | tf_op jit(solution)/shard_map/all_to_all | solution.py:30
  33.8 3.0 %convolution_convert_fusion.11 = bf16[2,128,256]{2,1,0:T(8,128)(2,1)} fusion(bf16[2,128,4096]{2,1,0:T(8,128)(2,1)S(1)} %copy-done, bf16[4096,256,1]{1,0,2:T(8,128)(2,1)} %bitcast.61), kind=kOutput, calls=%fused_computation.364 | convolution fusion | flops 536936448 | bytes 4325376 | tf_op jit(solution)/shard_map/dot_general | solution.py:494
  36.8 196.1 %while.19 = (s32[]{:T(128)}, bf16[2,1152,128]{2,1,0:T(8,128)(2,1)}, bf16[2,1152,128]{2,1,0:T(8,128)(2,1)}, bf16[2,128,256]{2,1,0:T(8,128)(2,1)}, f32[2]{0:T(128)...) while((s32[]{:T(128)}, bf16[2,1152,128]{2,1,0:T(8,128)(2,1)}, ...), condition=%wide.region_22.23_spmd, body=%wide.region_0.22_spmd.sunk | while | flops 8245876736 | bytes 360802208 | solution.py:527
  37.0 1.2 dynamic_slice.78
  44.5 3.5 %fusion.458 = (f32[128]{0:T(128)S(1)}, f32[4096,128]{1,0:T(8,128)S(1)}) fusion(f32[6,128]{1,0:T(8,128)S(1)} %get-tuple-element.735, f32[3,4096]{1,0:T(4,128)S(1)} %fusion.456, f32[3,4096]{1,0:T(4,128)S(1)} %fusion.457), kind=kOutput, calls=%fused_computation.376.clone.1 | convolution fusion | flops 38297472 | bytes 2199040 | tf_op jit(solution)/shard_map/while/body/eval_jaxpr/kp,kc->pc/dot_general | solution.py:85
  51.5 3.0 %select_reduce_fusion.8 = (f32[128]{0:T(128)S(1)}, f32[64,8,9,128]{3,1,2,0:T(8,128)S(1)}) fusion(pred[8,9]{0,1:T(8,128)(4,1)S(1)} %get-tuple-element.749, bf16[3,3,128,128]{3,2,1,0:T(8,128)(2,1)S(1)} %bitcast.346, bf16[64,1,7,2,128]{4,2,3,0,1:T(8,128)(2,1)S(1)} %slice.187, bf16[64,1,8,9,128]{4,2,3,0,1:T(8,128)(2,1)S(1)} %copy.120), kind=kOutput, calls=%fused_computation.57.clone.1 | convolution fusion | flops 1350893440 | bytes 4063816 | tf_op jit(solution)/shard_map/while/body/eval_jaxpr/jvp()/conv_general_dilated | solution.py:115
  56.9 1.5 fusion.468
  59.4 3.1 %fusion.470 = f32[64,8,9,128]{3,1,2,0:T(8,128)S(1)} fusion(bf16[3,3,128,128]{3,2,1,0:T(8,128)(2,1)S(1)} %bitcast.347, bf16[64,1,8,1,128]{4,2,3,0,1:T(8,128)(2,1)S(1)} %pad.313, bf16[64,1,8,9,128]{4,2,3,0,1:T(8,128)(2,1)S(1)} %fusion.468, bf16[64,1,8,1,128]{4,2,3,0,1:T(8,128)(2,1)S(1)} %pad.314), kind=kOutput, calls=%fused_computation.93.clone.1 | convolution fusion | flops 1349124096 | bytes 4096000 | tf_op jit(solution)/shard_map/while/body/eval_jaxpr/jvp()/conv_general_dilated | solution.py:115
  63.1 1.2 copy.122
  69.2 2.1 convert_reduce_fusion.5
  71.3 1.4 convolution_convert_fusion.21
  73.6 2.1 convert_reduce_fusion.4
  76.7 1.5 convolution_convert_fusion.20
  78.1 4.4 %multiply_reduce_fusion.14 = (f32[]{:T(128)}, f32[3,4096]{1,0:T(4,128)}) fusion(f32[1,3,4096]{2,0,1:T(1,128)S(1)} %constant_dynamic-slice_fusion.8, bf16[3,128]{1,0:T(4,128)(2,1)} %get-tuple-element.743, f32[4096,128]{1,0:T(8,128)} %copy-done.1, bf16[128,128]{1,0:T(8,128)(2,1)} %get-tuple-element.742, ...), kind=kOutput, calls=%fused_computation.200.clone.1 | convolution fusion | flops 140546048 | bytes 3277572 | tf_op jit(solution)/shard_map/while/body/eval_jaxpr/jvp(kc,pc->kp)/dot_general | solution.py:164
  82.5 1.7 convolution_convert_fusion.22
  85.2 1.2 convolution_convert_fusion.23
  95.0 1.6 copy.130
  96.6 1.6 constant_dynamic-update-slice_fusion.6
  98.2 2.2 convolution_convert_fusion.25
  102.0 1.5 multiply_reduce_fusion.17
  108.5 4.2 %select_reduce_fusion.10 = (f32[128]{0:T(128)S(1)}, f32[64,8,9,128]{3,1,2,0:T(8,128)S(1)}) fusion(f32[64,8,9,128]{3,1,2,0:T(8,128)S(1)} %copy-done.8, f32[128]{0:T(128)S(1)} %copy-done.47, pred[8,9]{0,1:T(8,128)(4,1)S(1)} %copy-done.37, f32[128]{0:T(128)S(1)} %copy-done.54, f32[128]{0:T(128)S(1)} %copy-done.52, f32[128]{0:T(128)S(1)} %copy-done.56, ...), kind=kOutput, calls=%fused_computation.51.clone.1 | convolution fusion | flops 1360920448 | bytes 6425160 | tf_op jit(solution)/shard_map/while/body/eval_jaxpr/transpose(jvp())/conv_general_dilated | solution.py:115
  117.0 4.3 %fusion.493 = bf16[3,3,128,128,1]{3,2,1,4,0:T(8,128)(2,1)S(1)} fusion(bf16[64,8,9,128,1]{3,1,4,2,0:T(8,128)(2,1)S(1)} %fusion.489, bf16[64,8,9,128,1]{3,1,4,2,0:T(8,128)(2,1)S(1)} %copy.126, bf16[64,8,9,128,1]{3,1,4,2,0:T(8,128)(2,1)S(1)} %fusion.490, f32[128]{0:T(128)S(1)} %fusion.492, pred[8,9]{0,1:T(8,128)(4,1)S(1)} %copy-done.38, ...), kind=kOutput, calls=%fused_computation.101.clone.1 | convolution fusion | flops 1360281600 | bytes 8554568 | tf_op jit(solution)/shard_map/while/body/eval_jaxpr/transpose(jvp())/conv_general_dilated | solution.py:115
  123.8 5.0 %fusion.486 = bf16[3,3,128,128,1]{3,2,1,4,0:T(8,128)(2,1)S(1)} fusion(bf16[64,8,9,128,1]{3,0,2,1,4:T(8,128)(2,1)S(1)} %bitcast.336, bf16[64,8,9,128,1]{3,1,2,0,4:T(8,128)(2,1)S(1)} %maximum_bitcast_fusion.8, bf16[64,8,9,128,1]{3,1,2,0,4:T(8,128)(2,1)S(1)} %fusion.485, bf16[64,8,9,128,1]{3,1,2,0,4:T(8,128)(2,1)S(1)} %maximum_bitcast_fusion.9), kind=kOutput, calls=%fused_computation.100.clone.1 | convolution fusion | flops 1348337664 | bytes 5013504 | tf_op jit(solution)/shard_map/while/body/eval_jaxpr/transpose(jvp())/conv_general_dilated | solution.py:115
  133.7 1.2 dynamic_slice.78
  141.1 3.5 %fusion.458 = (f32[128]{0:T(128)S(1)}, f32[4096,128]{1,0:T(8,128)S(1)}) fusion(f32[6,128]{1,0:T(8,128)S(1)} %get-tuple-element.735, f32[3,4096]{1,0:T(4,128)S(1)} %fusion.456, f32[3,4096]{1,0:T(4,128)S(1)} %fusion.457), kind=kOutput, calls=%fused_computation.376.clone.1 | convolution fusion | flops 38297472 | bytes 2199040 | tf_op jit(solution)/shard_map/while/body/eval_jaxpr/kp,kc->pc/dot_general | solution.py:85
  148.2 3.0 %select_reduce_fusion.8 = (f32[128]{0:T(128)S(1)}, f32[64,8,9,128]{3,1,2,0:T(8,128)S(1)}) fusion(pred[8,9]{0,1:T(8,128)(4,1)S(1)} %get-tuple-element.749, bf16[3,3,128,128]{3,2,1,0:T(8,128)(2,1)S(1)} %bitcast.346, bf16[64,1,7,2,128]{4,2,3,0,1:T(8,128)(2,1)S(1)} %slice.187, bf16[64,1,8,9,128]{4,2,3,0,1:T(8,128)(2,1)S(1)} %copy.120), kind=kOutput, calls=%fused_computation.57.clone.1 | convolution fusion | flops 1350893440 | bytes 4063816 | tf_op jit(solution)/shard_map/while/body/eval_jaxpr/jvp()/conv_general_dilated | solution.py:115
  153.5 1.2 fusion.468
  155.7 3.1 %fusion.470 = f32[64,8,9,128]{3,1,2,0:T(8,128)S(1)} fusion(bf16[3,3,128,128]{3,2,1,0:T(8,128)(2,1)S(1)} %bitcast.347, bf16[64,1,8,1,128]{4,2,3,0,1:T(8,128)(2,1)S(1)} %pad.313, bf16[64,1,8,9,128]{4,2,3,0,1:T(8,128)(2,1)S(1)} %fusion.468, bf16[64,1,8,1,128]{4,2,3,0,1:T(8,128)(2,1)S(1)} %pad.314), kind=kOutput, calls=%fused_computation.93.clone.1 | convolution fusion | flops 1349124096 | bytes 4096000 | tf_op jit(solution)/shard_map/while/body/eval_jaxpr/jvp()/conv_general_dilated | solution.py:115
  159.5 1.2 copy.122
  165.5 2.1 convert_reduce_fusion.5
  167.6 1.4 convolution_convert_fusion.21
  169.9 2.1 convert_reduce_fusion.4
  173.0 1.5 convolution_convert_fusion.20
  174.5 4.4 %multiply_reduce_fusion.14 = (f32[]{:T(128)}, f32[3,4096]{1,0:T(4,128)}) fusion(f32[1,3,4096]{2,0,1:T(1,128)S(1)} %constant_dynamic-slice_fusion.8, bf16[3,128]{1,0:T(4,128)(2,1)} %get-tuple-element.743, f32[4096,128]{1,0:T(8,128)} %copy-done.1, bf16[128,128]{1,0:T(8,128)(2,1)} %get-tuple-element.742, ...), kind=kOutput, calls=%fused_computation.200.clone.1 | convolution fusion | flops 140546048 | bytes 3277572 | tf_op jit(solution)/shard_map/while/body/eval_jaxpr/jvp(kc,pc->kp)/dot_general | solution.py:164
  178.8 1.9 convolution_convert_fusion.22
  191.5 1.6 copy.130
  193.1 1.6 constant_dynamic-update-slice_fusion.6
  194.8 2.2 convolution_convert_fusion.25
  198.6 1.5 multiply_reduce_fusion.17
  205.0 4.2 %select_reduce_fusion.10 = (f32[128]{0:T(128)S(1)}, f32[64,8,9,128]{3,1,2,0:T(8,128)S(1)}) fusion(f32[64,8,9,128]{3,1,2,0:T(8,128)S(1)} %copy-done.8, f32[128]{0:T(128)S(1)} %copy-done.47, pred[8,9]{0,1:T(8,128)(4,1)S(1)} %copy-done.37, f32[128]{0:T(128)S(1)} %copy-done.54, f32[128]{0:T(128)S(1)} %copy-done.52, f32[128]{0:T(128)S(1)} %copy-done.56, ...), kind=kOutput, calls=%fused_computation.51.clone.1 | convolution fusion | flops 1360920448 | bytes 6425160 | tf_op jit(solution)/shard_map/while/body/eval_jaxpr/transpose(jvp())/conv_general_dilated | solution.py:115
  213.5 4.3 %fusion.493 = bf16[3,3,128,128,1]{3,2,1,4,0:T(8,128)(2,1)S(1)} fusion(bf16[64,8,9,128,1]{3,1,4,2,0:T(8,128)(2,1)S(1)} %fusion.489, bf16[64,8,9,128,1]{3,1,4,2,0:T(8,128)(2,1)S(1)} %copy.126, bf16[64,8,9,128,1]{3,1,4,2,0:T(8,128)(2,1)S(1)} %fusion.490, f32[128]{0:T(128)S(1)} %fusion.492, pred[8,9]{0,1:T(8,128)(4,1)S(1)} %copy-done.38, ...), kind=kOutput, calls=%fused_computation.101.clone.1 | convolution fusion | flops 1360281600 | bytes 8554568 | tf_op jit(solution)/shard_map/while/body/eval_jaxpr/transpose(jvp())/conv_general_dilated | solution.py:115
  220.3 4.8 %fusion.486 = bf16[3,3,128,128,1]{3,2,1,4,0:T(8,128)(2,1)S(1)} fusion(bf16[64,8,9,128,1]{3,0,2,1,4:T(8,128)(2,1)S(1)} %bitcast.336, bf16[64,8,9,128,1]{3,1,2,0,4:T(8,128)(2,1)S(1)} %maximum_bitcast_fusion.8, bf16[64,8,9,128,1]{3,1,2,0,4:T(8,128)(2,1)S(1)} %fusion.485, bf16[64,8,9,128,1]{3,1,2,0,4:T(8,128)(2,1)S(1)} %maximum_bitcast_fusion.9), kind=kOutput, calls=%fused_computation.100.clone.1 | convolution fusion | flops 1348337664 | bytes 5013504 | tf_op jit(solution)/shard_map/while/body/eval_jaxpr/transpose(jvp())/conv_general_dilated | solution.py:115
  232.9 1.3 reduce.4
  234.4 1.3 reduce.5
  238.0 1.3 fusion.283.conv_ref
  239.3 38.3 %finish.1 = (f32[9,128]{1,0:T(8,128)S(1)}, f32[9,128]{1,0:T(8,128)S(1)}, f32[4,2048]{1,0:T(4,128)S(1)}, f32[1,128]{1,0:T(1,128)S(1)}) custom-call(bf16[256,4096]{1,0:T(8,128)(2,1)S(1)} %bitcast.326, bf16[256,256]{1,0:T(8,128)(2,1)S(1)} %bitcast.349, bf16[2,4,4,4,16,256]{5,4,3,2,1,0:T(8,128)(2,1)S(1)} %fusion.283.conv_ref, ...), custom_call_target="tpu_custom_call" | custom-call | flops 3000000000 | bytes 8000000 | tf_op jit(solution)/shard_map/finish/pallas_call | solution.py:425
  (474 shorter events, 89.8 us)
Async XLA Ops:
  3.3 30.4 %copy-start = (bf16[2,128,4096]{2,1,0:T(8,128)(2,1)S(1)}, bf16[2,128,4096]{2,1,0:T(8,128)(2,1)}, u32[]{:S(2)}) copy-start(bf16[2,128,4096]{2,1,0:T(8,128)(2,1)} %param.25) | copy-start | bytes 6291460
  3.3 30.4 %all-to-all-start = ((bf16[2,2048,256]{2,1,0:T(8,128)(2,1)}), bf16[2,2048,256]{2,1,0:T(8,128)(2,1)}, u32[]{:S(2)}, u32[]{:S(2)}) async-start(bf16[2,2048,256]{2,1,0:T(8,128)(2,1)} %broadcast_in_dim.140), calls=%async_computation | async-start | bytes 4194304 | tf_op jit(solution)/shard_map/all_to_all | solution.py:30
  33.8 3.0 %copy-start.59 = (f32[6,128]{1,0:T(8,128)S(1)}, f32[6,128]{1,0:T(8,128)}, u32[]{:S(2)}) copy-start(f32[6,128]{1,0:T(8,128)} %param.26) | copy-start | bytes 9220
  47.9 17.8 %copy-start.72 = (s32[128]{0:T(128)}, s32[128]{0:T(128)S(1)}, u32[]{:S(2)}) copy-start(s32[128]{0:T(128)S(1)} %and_select_fusion.2) | copy-start | bytes 1540 | tf_op jit(solution)/shard_map/while
  54.6 3.8 %copy-start.7 = (f32[64,8,9,128]{3,1,2,0:T(8,128)}, f32[64,8,9,128]{3,1,2,0:T(8,128)S(1)}, u32[]{:S(2)}) copy-start(f32[64,8,9,128]{3,1,2,0:T(8,128)S(1)} %get-tuple-element.625) | copy-start | bytes 7077892 | tf_op jit(solution)/shard_map/while
  54.8 3.6 %copy-start.46 = (f32[128]{0:T(128)}, f32[128]{0:T(128)S(1)}, u32[]{:S(2)}) copy-start(f32[128]{0:T(128)S(1)} %convolution_bitcast_fusion.15) | copy-start | bytes 1540 | tf_op jit(solution)/shard_map/while
  58.4 4.0 %copy-start.9 = (bf16[64,1,8,9,128]{4,2,3,0,1:T(8,128)(2,1)}, bf16[64,1,8,9,128]{4,2,3,0,1:T(8,128)(2,1)S(1)}, u32[]{:S(2)}) copy-start(bf16[64,1,8,9,128]{4,2,3,0,1:T(8,128)(2,1)S(1)} %fusion.468) | copy-start | bytes 3538948 | tf_op jit(solution)/shard_map/while
  67.0 5.7 %copy-start.20 = (bf16[4096,128]{0,1:T(8,128)(2,1)}, bf16[4096,128]{0,1:T(8,128)(2,1)S(1)}, u32[]{:S(2)}) copy-start(bf16[4096,128]{0,1:T(8,128)(2,1)S(1)} %fusion.473) | copy-start | bytes 3145732 | tf_op jit(solution)/shard_map/while
  68.4 4.3 %copy-start.48 = (pred[128]{0:T(512)(128)(4,1)}, pred[128]{0:T(512)(128)(4,1)S(1)}, u32[]{:S(2)}) copy-start(pred[128]{0:T(512)(128)(4,1)S(1)} %iota_compare_fusion.8) | copy-start | bytes 388 | tf_op jit(solution)/shard_map/while
  69.2 3.6 %copy-start.27 = (f32[4096]{0:T(1024)}, f32[4096]{0:T(1024)S(1)}, u32[]{:S(2)}) copy-start(f32[4096]{0:T(1024)S(1)} %fusion.477) | copy-start | bytes 49156 | tf_op jit(solution)/shard_map/while
  73.5 4.6 %copy-start.29 = (f32[4096]{0:T(1024)}, f32[4096]{0:T(1024)S(1)}, u32[]{:S(2)}) copy-start(f32[4096]{0:T(1024)S(1)} %fusion.475) | copy-start | bytes 49156 | tf_op jit(solution)/shard_map/while
  82.5 3.9 %copy-start.30 = (f32[4096]{0:T(1024)S(1)}, f32[4096]{0:T(1024)}, u32[]{:S(2)}) copy-start(f32[4096]{0:T(1024)} %copy-done.29) | copy-start | bytes 49156 | tf_op jit(solution)/shard_map/while
  82.5 3.9 %copy-start.6 = (f32[4096,128]{0,1:T(8,128)S(1)}, f32[4096,128]{0,1:T(8,128)}, u32[]{:S(2)}) copy-start(f32[4096,128]{0,1:T(8,128)} %copy-done.5) | copy-start | bytes 6291460 | tf_op jit(solution)/shard_map/while
  87.7 3.1 %copy-start.17 = (f32[4096,128]{0,1:T(8,128)}, f32[4096,128]{0,1:T(8,128)S(1)}, u32[]{:S(2)}) copy-start(f32[4096,128]{0,1:T(8,128)S(1)} %get-tuple-element.648) | copy-start | bytes 6291460 | tf_op jit(solution)/shard_map/while
  93.4 4.8 %copy-start.50 = (pred[128]{0:T(512)(128)(4,1)S(1)}, pred[128]{0:T(512)(128)(4,1)}, u32[]{:S(2)}) copy-start(pred[128]{0:T(512)(128)(4,1)} %copy-done.48) | copy-start | bytes 388 | tf_op jit(solution)/shard_map/while
  96.6 3.8 %copy-start.19 = (f32[4096,128]{0,1:T(8,128)S(1)}, f32[4096,128]{0,1:T(8,128)}, u32[]{:S(2)}) copy-start(f32[4096,128]{0,1:T(8,128)} %copy-done.18) | copy-start | bytes 6291460 | tf_op jit(solution)/shard_map/while
  96.6 3.8 %copy-start.23 = (pred[4096,128]{0,1:T(32,128)(4,1)S(1)}, pred[4096,128]{0,1:T(32,128)(4,1)}, u32[]{:S(2)}) copy-start(pred[4096,128]{0,1:T(32,128)(4,1)} %get-tuple-element.643) | copy-start | bytes 1572868 | tf_op jit(solution)/shard_map/while
  108.5 4.2 %copy-start.74 = (f32[128]{0:T(128)S(1)}, f32[128]{0:T(128)}, u32[]{:S(2)}) copy-start(f32[128]{0:T(128)} %get-tuple-element.665) | copy-start | bytes 1540 | tf_op jit(solution)/shard_map/while
  123.7 5.1 %copy-start.40 = (bf16[2,1152,128]{2,1,0:T(8,128)(2,1)S(1)}, bf16[2,1152,128]{2,1,0:T(8,128)(2,1)}, u32[]{:S(2)}) copy-start(bf16[2,1152,128]{2,1,0:T(8,128)(2,1)} %get-tuple-element.698) | copy-start | bytes 1769476 | tf_op jit(solution)/shard_map/while
  123.8 5.1 %copy-start.42 = (bf16[2,1152,128]{2,1,0:T(8,128)(2,1)S(1)}, bf16[2,1152,128]{2,1,0:T(8,128)(2,1)}, u32[]{:S(2)}) copy-start(bf16[2,1152,128]{2,1,0:T(8,128)(2,1)} %get-tuple-element.699) | copy-start | bytes 1769476 | tf_op jit(solution)/shard_map/while
  123.8 5.2 %copy-start.69 = (f32[2]{0:T(128)S(1)}, f32[2]{0:T(128)}, u32[]{:S(2)}) copy-start(f32[2]{0:T(128)} %get-tuple-element.701) | copy-start | bytes 28 | tf_op jit(solution)/shard_map/while
  123.8 6.5 %copy-start.33 = (bf16[128,128]{1,0:T(8,128)(2,1)S(1)}, bf16[128,128]{1,0:T(8,128)(2,1)}, u32[]{:S(2)}) copy-start(bf16[128,128]{1,0:T(8,128)(2,1)} %get-tuple-element.788) | copy-start | bytes 98308 | tf_op jit(solution)/shard_map/while
  123.8 6.5 %copy-start.60 = (f32[6,128]{1,0:T(8,128)S(1)}, f32[6,128]{1,0:T(8,128)}, u32[]{:S(2)}) copy-start(f32[6,128]{1,0:T(8,128)} %get-tuple-element.847) | copy-start | bytes 9220 | tf_op jit(solution)/shard_map/while
  123.8 6.5 %copy-start.66 = (s32[2]{0:T(128)S(1)}, s32[2]{0:T(128)}, u32[]{:S(2)}) copy-start(s32[2]{0:T(128)} %get-tuple-element.878) | copy-start | bytes 28 | tf_op jit(solution)/shard_map/while
  123.8 6.5 %copy-start.68 = (s32[2]{0:T(128)S(1)}, s32[2]{0:T(128)}, u32[]{:S(2)}) copy-start(s32[2]{0:T(128)} %get-tuple-element.910) | copy-start | bytes 28 | tf_op jit(solution)/shard_map/while
  144.6 17.5 %copy-start.72 = (s32[128]{0:T(128)}, s32[128]{0:T(128)S(1)}, u32[]{:S(2)}) copy-start(s32[128]{0:T(128)S(1)} %and_select_fusion.2) | copy-start | bytes 1540 | tf_op jit(solution)/shard_map/while
  151.2 3.5 %copy-start.7 = (f32[64,8,9,128]{3,1,2,0:T(8,128)}, f32[64,8,9,128]{3,1,2,0:T(8,128)S(1)}, u32[]{:S(2)}) copy-start(f32[64,8,9,128]{3,1,2,0:T(8,128)S(1)} %get-tuple-element.625) | copy-start | bytes 7077892 | tf_op jit(solution)/shard_map/while
  151.4 3.3 %copy-start.46 = (f32[128]{0:T(128)}, f32[128]{0:T(128)S(1)}, u32[]{:S(2)}) copy-start(f32[128]{0:T(128)S(1)} %convolution_bitcast_fusion.15) | copy-start | bytes 1540 | tf_op jit(solution)/shard_map/while
  154.7 4.0 %copy-start.9 = (bf16[64,1,8,9,128]{4,2,3,0,1:T(8,128)(2,1)}, bf16[64,1,8,9,128]{4,2,3,0,1:T(8,128)(2,1)S(1)}, u32[]{:S(2)}) copy-start(bf16[64,1,8,9,128]{4,2,3,0,1:T(8,128)(2,1)S(1)} %fusion.468) | copy-start | bytes 3538948 | tf_op jit(solution)/shard_map/while
  163.4 5.7 %copy-start.20 = (bf16[4096,128]{0,1:T(8,128)(2,1)}, bf16[4096,128]{0,1:T(8,128)(2,1)S(1)}, u32[]{:S(2)}) copy-start(bf16[4096,128]{0,1:T(8,128)(2,1)S(1)} %fusion.473) | copy-start | bytes 3145732 | tf_op jit(solution)/shard_map/while
  164.7 4.3 %copy-start.48 = (pred[128]{0:T(512)(128)(4,1)}, pred[128]{0:T(512)(128)(4,1)S(1)}, u32[]{:S(2)}) copy-start(pred[128]{0:T(512)(128)(4,1)S(1)} %iota_compare_fusion.8) | copy-start | bytes 388 | tf_op jit(solution)/shard_map/while
  165.5 3.6 %copy-start.27 = (f32[4096]{0:T(1024)}, f32[4096]{0:T(1024)S(1)}, u32[]{:S(2)}) copy-start(f32[4096]{0:T(1024)S(1)} %fusion.477) | copy-start | bytes 49156 | tf_op jit(solution)/shard_map/while
  169.9 4.6 %copy-start.29 = (f32[4096]{0:T(1024)}, f32[4096]{0:T(1024)S(1)}, u32[]{:S(2)}) copy-start(f32[4096]{0:T(1024)S(1)} %fusion.475) | copy-start | bytes 49156 | tf_op jit(solution)/shard_map/while
  178.8 4.1 %copy-start.30 = (f32[4096]{0:T(1024)S(1)}, f32[4096]{0:T(1024)}, u32[]{:S(2)}) copy-start(f32[4096]{0:T(1024)} %copy-done.29) | copy-start | bytes 49156 | tf_op jit(solution)/shard_map/while
  178.8 4.1 %copy-start.6 = (f32[4096,128]{0,1:T(8,128)S(1)}, f32[4096,128]{0,1:T(8,128)}, u32[]{:S(2)}) copy-start(f32[4096,128]{0,1:T(8,128)} %copy-done.5) | copy-start | bytes 6291460 | tf_op jit(solution)/shard_map/while
  184.2 3.1 %copy-start.17 = (f32[4096,128]{0,1:T(8,128)}, f32[4096,128]{0,1:T(8,128)S(1)}, u32[]{:S(2)}) copy-start(f32[4096,128]{0,1:T(8,128)S(1)} %get-tuple-element.648) | copy-start | bytes 6291460 | tf_op jit(solution)/shard_map/while
  189.9 4.8 %copy-start.50 = (pred[128]{0:T(512)(128)(4,1)S(1)}, pred[128]{0:T(512)(128)(4,1)}, u32[]{:S(2)}) copy-start(pred[128]{0:T(512)(128)(4,1)} %copy-done.48) | copy-start | bytes 388 | tf_op jit(solution)/shard_map/while
  193.1 3.8 %copy-start.19 = (f32[4096,128]{0,1:T(8,128)S(1)}, f32[4096,128]{0,1:T(8,128)}, u32[]{:S(2)}) copy-start(f32[4096,128]{0,1:T(8,128)} %copy-done.18) | copy-start | bytes 6291460 | tf_op jit(solution)/shard_map/while
  193.1 3.8 %copy-start.23 = (pred[4096,128]{0,1:T(32,128)(4,1)S(1)}, pred[4096,128]{0,1:T(32,128)(4,1)}, u32[]{:S(2)}) copy-start(pred[4096,128]{0,1:T(32,128)(4,1)} %get-tuple-element.643) | copy-start | bytes 1572868 | tf_op jit(solution)/shard_map/while
  205.0 4.2 %copy-start.74 = (f32[128]{0:T(128)S(1)}, f32[128]{0:T(128)}, u32[]{:S(2)}) copy-start(f32[128]{0:T(128)} %get-tuple-element.665) | copy-start | bytes 1540 | tf_op jit(solution)/shard_map/while
  220.3 4.9 %copy-start.40 = (bf16[2,1152,128]{2,1,0:T(8,128)(2,1)S(1)}, bf16[2,1152,128]{2,1,0:T(8,128)(2,1)}, u32[]{:S(2)}) copy-start(bf16[2,1152,128]{2,1,0:T(8,128)(2,1)} %get-tuple-element.698) | copy-start | bytes 1769476 | tf_op jit(solution)/shard_map/while
  220.3 4.9 %copy-start.42 = (bf16[2,1152,128]{2,1,0:T(8,128)(2,1)S(1)}, bf16[2,1152,128]{2,1,0:T(8,128)(2,1)}, u32[]{:S(2)}) copy-start(bf16[2,1152,128]{2,1,0:T(8,128)(2,1)} %get-tuple-element.699) | copy-start | bytes 1769476 | tf_op jit(solution)/shard_map/while
  220.3 5.0 %copy-start.69 = (f32[2]{0:T(128)S(1)}, f32[2]{0:T(128)}, u32[]{:S(2)}) copy-start(f32[2]{0:T(128)} %get-tuple-element.701) | copy-start | bytes 28 | tf_op jit(solution)/shard_map/while
  220.3 6.3 %copy-start.33 = (bf16[128,128]{1,0:T(8,128)(2,1)S(1)}, bf16[128,128]{1,0:T(8,128)(2,1)}, u32[]{:S(2)}) copy-start(bf16[128,128]{1,0:T(8,128)(2,1)} %get-tuple-element.788) | copy-start | bytes 98308 | tf_op jit(solution)/shard_map/while
  220.3 6.3 %copy-start.60 = (f32[6,128]{1,0:T(8,128)S(1)}, f32[6,128]{1,0:T(8,128)}, u32[]{:S(2)}) copy-start(f32[6,128]{1,0:T(8,128)} %get-tuple-element.847) | copy-start | bytes 9220 | tf_op jit(solution)/shard_map/while
  220.3 6.3 %copy-start.66 = (s32[2]{0:T(128)S(1)}, s32[2]{0:T(128)}, u32[]{:S(2)}) copy-start(s32[2]{0:T(128)} %get-tuple-element.878) | copy-start | bytes 28 | tf_op jit(solution)/shard_map/while
  220.3 6.3 %copy-start.68 = (s32[2]{0:T(128)S(1)}, s32[2]{0:T(128)}, u32[]{:S(2)}) copy-start(s32[2]{0:T(128)} %get-tuple-element.910) | copy-start | bytes 28 | tf_op jit(solution)/shard_map/while
  235.9 3.4 %copy-start.64 = (bf16[2,128,256]{2,1,0:T(8,128)(2,1)S(1)}, bf16[2,128,256]{2,1,0:T(8,128)(2,1)}, u32[]{:S(2)}) copy-start(bf16[2,128,256]{2,1,0:T(8,128)(2,1)} %get-tuple-element.882) | copy-start | bytes 393220
  (97 other events, 152.4 us)

commit v2 on v1

--- a/solution.py
+++ b/solution.py
@@ -3,6 +3,7 @@
 
 import jax
 import jax.numpy as jnp
+import numpy as np
 from jax import lax
 from jax.sharding import Mesh
 from jax.sharding import PartitionSpec as P
@@ -19,153 +20,462 @@
 DP = ("dp_0", "dp_1", "dp_2", "dp_3")
 
 
-def in_order(tiles, dim):
-    tiles = jnp.moveaxis(tiles, 0, dim)
-    dims = tiles.shape
-    return tiles.reshape(*dims[:dim], dims[dim] * dims[dim + 1], *dims[dim + 2 :])
-
-
-def from_everyone(array, axis):
-    copies = jnp.broadcast_to(array, (lax.axis_size(axis), *array.shape))
-    return lax.all_to_all(copies, axis, split_axis=0, concat_axis=0, tiled=True)
-
-
-def gather_directly(array, axis, dim):
-    return in_order(from_everyone(array, axis), dim)
-
-
-def split_up(array, dim, count):
-    dims = array.shape
-    tiles = array.reshape(*dims[:dim], count, dims[dim] // count, *dims[dim + 1 :])
-    return jnp.moveaxis(tiles, dim, 0)
-
-
-def sum_together(arrays, axis, dims):
-    count = lax.axis_size(axis)
-    tiles = [split_up(a, dim, count) for a, dim in zip(arrays, dims)]
-    lines = jnp.concatenate([b.reshape(count, -1) for b in tiles], axis=1)
-    width = max(16, -(-lines.shape[1] // 1024) * 8)
-    lines = jnp.pad(lines, ((0, 0), (0, width * 128 - lines.shape[1]))).reshape(-1, 128)
-    line, at, finished = (lax.psum_scatter(lines, axis, tiled=True).reshape(-1), 0, [])
-    for b in tiles:
-        part = b[0]
-        finished.append(line[at : at + part.size].reshape(part.shape))
-        at += part.size
-    return tuple(finished)
-
-
-def sent_and_summed(array, axis, dim):
-    tiles = split_up(array, dim, lax.axis_size(axis))
-    arrived = lax.all_to_all(tiles, axis, split_axis=0, concat_axis=0, tiled=True)
-    return arrived.sum(axis=0)
-
-
-def over_axes(array, axes):
-    return functools.reduce(lax.psum, axes, array)
-
-
 def signal_level(index):
     ratio = (index.astype(jnp.float32) / STEPS + 0.008) / 1.008
     cosine = jnp.cos(ratio * (math.pi / 2.0))
     return cosine * cosine
 
 
-def sinusoid(index):
-    freqs = jnp.exp(-math.log(10000.0) * jnp.arange(FREQS, dtype=jnp.float32) / FREQS)
-    angles = index.astype(jnp.float32) * freqs
-    return jnp.concatenate([jnp.sin(angles), jnp.cos(angles)])
-
-
-def prepare(clean, noise, lowres, aug_noise, tstep, level, w_stem, w_time):
-    signal = signal_level(tstep)
-    aug_signal = signal_level(level)
-    noisy = jnp.sqrt(signal) * clean + jnp.sqrt(1.0 - signal) * noise
-    low_noisy = jnp.sqrt(aug_signal) * lowres + jnp.sqrt(1.0 - aug_signal) * aug_noise
-    stacked = jnp.concatenate([noisy, low_noisy], axis=0)
-    h_start = jnp.einsum("kp,kc->pc", stacked, w_stem, precision=lax.Precision.HIGHEST)
-    feature = jnp.concatenate([sinusoid(tstep), sinusoid(level)])[None, :]
-    embed = jax.nn.silu(jnp.dot(feature, w_time, precision=lax.Precision.HIGHEST))[0]
-    channels = w_stem.shape[1]
-    return (h_start, embed[:channels], embed[channels:])
-
-
-def group_matrix(channels):
-    members = channels // GROUPS
-    labels = jnp.arange(channels) // members
-    return (labels[:, None] == labels[None, :]).astype(jnp.float32) / members
-
-
-def group_norm(values, grouping):
-    average = jnp.dot(
-        jnp.mean(values, axis=0, keepdims=True), grouping, precision=lax.Precision.HIGHEST
-    )
-    centred = values - average
-    spread = jnp.dot(
-        jnp.mean(centred * centred, axis=0, keepdims=True),
-        grouping,
+PIXELS = S * S
+CHUNK = 512
+CHUNKS = PIXELS // CHUNK
+EDGE = S
+C = 128
+
+
+def group_total(line):
+    lane = lax.broadcasted_iota(jnp.int32, line.shape, 1)
+    pair = line + jnp.where(
+        lane % 2 == 0, pltpu.roll(line, C - 1, 1), pltpu.roll(line, 1, 1)
+    )
+    return pair + jnp.where(
+        lane % 4 < 2, pltpu.roll(pair, C - 2, 1), pltpu.roll(pair, 2, 1)
+    )
+
+
+def group_mean(total):
+    line = jnp.broadcast_to(jnp.sum(total, axis=0, keepdims=True), (8, C)) / PIXELS
+    return group_total(line)[0:1] / (C // GROUPS)
+
+
+def row_of(value, i):
+    row = value[0:1]
+    for r in range(1, value.shape[0]):
+        row = jnp.where(i == r, value[r : r + 1], row)
+    return row
+
+
+def fold(value):
+    return jnp.sum(value.reshape(-1, 8, value.shape[-1]), axis=0)
+
+
+def spread(act):
+    column = lax.broadcasted_iota(jnp.int32, act.shape, 0) % S
+    rows = act.shape[0]
+    left = jnp.where(column == 0, 0.0, pltpu.roll(act, 1, 0))
+    right = jnp.where(column == S - 1, 0.0, pltpu.roll(act, rows - 1, 0))
+    return jnp.concatenate(
+        [left.astype(jnp.bfloat16), act.astype(jnp.bfloat16), right.astype(jnp.bfloat16)], axis=1
+    )
+
+
+def span(j, size=CHUNK):
+    return pl.ds(pl.multiple_of(j * size, size), size)
+
+
+def shifted(j, dy, size=CHUNK):
+    return pl.ds(pl.multiple_of(j * size + dy * S, S), size)
+
+
+def clear_edges(ref, i):
+    zero = jnp.zeros((EDGE, 3 * C), jnp.bfloat16)
+    ref[i, :EDGE] = zero
+    ref[i, EDGE + PIXELS :] = zero
+
+
+def conv_rows(wide_ref, i, j, weight_ref):
+    rows = jnp.concatenate([wide_ref[i, shifted(j, dy)] for dy in range(3)], axis=1)
+    return jnp.dot(rows, weight_ref[...], preferred_element_type=jnp.float32)
+
+
+def loop_sum(body, width=C):
+    return lax.fori_loop(0, CHUNKS, body, jnp.zeros((8, width), jnp.float32))
+
+
+def forward_kernel(
+    coef_ref,
+    clean_ref,
+    noise_ref,
+    low_ref,
+    aug_ref,
+    stem_ref,
+    feature_ref,
+    time_ref,
+    one_ref,
+    two_ref,
+    mid_ref,
+    out_ref,
+    wide_one,
+    wide_two,
+    stats_ref,
+    planes_ref,
+    stems_ref,
+    embed_ref,
+    lhs_ref,
+):
+    images = clean_ref.shape[1]
+    w = jnp.concatenate([stem_ref[...], jnp.zeros((2, C), jnp.float32)], axis=0)
+    w1 = w.astype(jnp.bfloat16).astype(jnp.float32)
+    w2 = (w - w1).astype(jnp.bfloat16).astype(jnp.float32)
+    w3 = w - w1 - w2
+    stems_ref[...] = jnp.concatenate([w1, w2, w1, w3, w2, w1], axis=0).astype(jnp.bfloat16)
+    feature = jnp.concatenate(
+        [feature_ref[...], jnp.zeros((8 - images, 2 * C), jnp.float32)], axis=0
+    )
+    embed = jnp.dot(
+        feature,
+        time_ref[...],
         precision=lax.Precision.HIGHEST,
-    )
-    return centred * lax.rsqrt(spread + 1e-05)
-
-
-def convolve(activation, weight):
-    channels = weight.shape[1]
-    kernel = weight.reshape(3, 3, channels, channels)
-    picture = activation.reshape(1, S, S, channels)
-    result = lax.conv_general_dilated(
-        picture,
-        kernel,
-        (1, 1),
-        "SAME",
-        dimension_numbers=("NHWC", "HWIO", "NHWC"),
         preferred_element_type=jnp.float32,
     )
-    return result.reshape(S * S, channels)
-
-
-def image_loss(
-    conv_one, conv_two, keys_values, h_start, scale, shift, keep, w_query, w_output, w_head, noise
-):
-    channels = conv_one.shape[1]
-    grouping = group_matrix(channels)
-    act_one = jax.nn.silu(group_norm(h_start, grouping)).astype(jnp.bfloat16)
-    conv_out_one = convolve(act_one, conv_one)
-    act_two = jax.nn.silu(group_norm(conv_out_one, grouping) * (1.0 + scale) + shift).astype(
-        jnp.bfloat16
-    )
-    h_mid = h_start + convolve(act_two, conv_two)
-    normed = group_norm(h_mid, grouping).astype(jnp.bfloat16)
-    queries = (
-        jnp.dot(normed, w_query, preferred_element_type=jnp.float32) * HEAD_DIM ** (-0.5)
-    ).astype(jnp.bfloat16)
-    width = w_query.shape[1]
-    pieces = []
-    for head_index in range(HEADS):
-        lower = head_index * HEAD_DIM
-        upper = lower + HEAD_DIM
-        scores = jnp.dot(
-            queries[:, lower:upper],
-            keys_values[:, lower:upper].T,
-            preferred_element_type=jnp.float32,
-        )
-        scores = jnp.where(keep[None, :], scores, -1e30)
-        highest = jnp.max(scores, axis=1, keepdims=True)
-        weights = jnp.exp(scores - highest)
-        probs = (weights / jnp.sum(weights, axis=1, keepdims=True)).astype(jnp.bfloat16)
-        pieces.append(
-            jnp.dot(
-                probs,
-                keys_values[:, width + lower : width + upper],
+    embed_ref[...] = embed * jax.nn.sigmoid(embed)
+    planes_ref[...] = jnp.zeros(planes_ref.shape, jnp.float32)
+
+    def image(i, carry):
+        for k in range(3):
+            planes_ref[k : k + 1] = (
+                coef_ref[i, 0] * row_of(clean_ref[k], i)
+                + coef_ref[i, 1] * row_of(noise_ref[k], i)
+            )
+            planes_ref[3 + k : 4 + k] = (
+                coef_ref[i, 2] * row_of(low_ref[k], i) + coef_ref[i, 3] * row_of(aug_ref[k], i)
+            )
+        s = planes_ref[...]
+        s1 = s.astype(jnp.bfloat16).astype(jnp.float32)
+        s2 = (s - s1).astype(jnp.bfloat16).astype(jnp.float32)
+        s3 = s - s1 - s2
+        lhs_ref[...] = jnp.concatenate([s1, s1, s2, s1, s2, s3], axis=0).astype(jnp.bfloat16)
+        clear_edges(wide_one, i)
+        clear_edges(wide_two, i)
+
+        def stem(j, total):
+            h = lax.dot_general(
+                lhs_ref[:, span(j)],
+                stems_ref[...],
+                (((0,), (0,)), ((), ())),
                 preferred_element_type=jnp.float32,
             )
+            mid_ref[i, span(j)] = h
+            return total + fold(h)
+
+        def variance(ref, mean):
+            def body(j, total):
+                centred = ref[i, span(j)] - mean
+                return total + fold(centred * centred)
+
+            return lax.rsqrt(group_mean(loop_sum(body)) + 1e-05)
+
+        mean_one = group_mean(loop_sum(stem))
+        inv_one = variance(mid_ref, mean_one)
+
+        def first(j, carry):
+            act = (mid_ref[i, span(j)] - mean_one) * inv_one
+            wide_one[i, shifted(j, 1)] = spread(act * jax.nn.sigmoid(act))
+            return carry
+
+        lax.fori_loop(0, CHUNKS, first, 0)
+
+        def conv_first(j, total):
+            value = conv_rows(wide_one, i, j, one_ref)
+            out_ref[i, span(j)] = value
+            return total + fold(value)
+
+        mean_two = group_mean(loop_sum(conv_first))
+        inv_two = variance(out_ref, mean_two)
+        gain = 1.0 + row_of(embed_ref[0:images, 0:C], i)
+        shift = row_of(embed_ref[0:images, C : 2 * C], i)
+
+        def next_act(j, carry):
+            act = (out_ref[i, span(j)] - mean_two) * inv_two * gain + shift
+            wide_two[i, shifted(j, 1)] = spread(act * jax.nn.sigmoid(act))
+            return carry
+
+        lax.fori_loop(0, CHUNKS, next_act, 0)
+
+        def conv_second(j, total):
+            value = mid_ref[i, span(j)] + conv_rows(wide_two, i, j, two_ref)
+            mid_ref[i, span(j)] = value
+            return total + fold(value)
+
+        mean_three = group_mean(loop_sum(conv_second))
+        inv_three = variance(mid_ref, mean_three)
+        stats_ref[i] = jnp.concatenate(
+            [mean_two, inv_two, mean_three, inv_three, gain, shift, gain, shift], axis=0
         )
-    attended = jnp.concatenate(pieces, axis=1).astype(jnp.bfloat16)
-    h_out = h_mid + jnp.dot(attended, w_output, preferred_element_type=jnp.float32)
-    pred = jnp.einsum(
-        "kc,pc->kp", w_head, h_out.astype(jnp.bfloat16), preferred_element_type=jnp.float32
-    )
-    error = pred - noise
-    return jnp.sum(error * error)
+        return carry
+
+    lax.fori_loop(0, images, image, 0)
+
+
+def forward(coefs, clean, noise, lowres, aug_noise, stem, feature, w_time, conv_one, conv_two):
+    images = clean.shape[1]
+    bf16, f32 = jnp.bfloat16, jnp.float32
+    wide = jax.ShapeDtypeStruct((images, PIXELS + 2 * EDGE, 3 * C), bf16)
+    flat = jax.ShapeDtypeStruct((images, PIXELS, C), f32)
+    return pl.pallas_call(
+        forward_kernel,
+        out_shape=(flat, flat, wide, wide, jax.ShapeDtypeStruct((images, 8, C), f32)),
+        in_specs=[pl.BlockSpec(memory_space=pltpu.SMEM)]
+        + [pl.BlockSpec(memory_space=pltpu.VMEM)] * 9,
+        out_specs=[pl.BlockSpec(memory_space=pltpu.VMEM)] * 5,
+        scratch_shapes=[
+            pltpu.VMEM((8, PIXELS), f32),
+            pltpu.VMEM((48, C), bf16),
+            pltpu.VMEM((8, 2 * C), f32),
+            pltpu.VMEM((48, PIXELS), bf16),
+        ],
+        compiler_params=pltpu.CompilerParams(vmem_limit_bytes=LIMIT_F * 2**20),
+        cost_estimate=pl.CostEstimate(
+            flops=10**10, bytes_accessed=22 * 10**6, transcendentals=2 * 10**6
+        ),
+        name="forward",
+    )(coefs, clean, noise, lowres, aug_noise, stem, feature, w_time, conv_one, conv_two)
+
+
+TN = (((0,), (0,)), ((), ()))
+NT = (((1,), (1,)), ((), ()))
+
+
+def mm(a, b, dims=(((1,), (0,)), ((), ()))):
+    return lax.dot_general(a, b, dims, preferred_element_type=jnp.float32)
+
+
+def backward_kernel(
+    half_ref,
+    lengths_ref,
+    noise_ref,
+    text_ref,
+    near_ref,
+    far_ref,
+    mid_ref,
+    out_ref,
+    wide_one,
+    wide_two,
+    stats_ref,
+    two_ref,
+    query_ref,
+    output_ref,
+    heads_ref,
+    cot_ref,
+    conv_ref,
+    loss_ref,
+    kv_ref,
+    key_ref,
+    val_ref,
+    dkey_ref,
+    dval_ref,
+    dnorm_ref,
+    dout_ref,
+    dhat_ref,
+    wide_grad,
+    grad_ref,
+    flat_ref,
+    total_ref,
+    flip_ref,
+    head_ref,
+    goal_ref,
+):
+    bf16, f32 = jnp.bfloat16, jnp.float32
+    images = noise_ref.shape[1]
+    tokens = text_ref.shape[0] // images
+    half = near_ref.shape[0]
+    mp = half_ref[0]
+    here = pl.ds(pl.multiple_of(mp * half, half), half)
+    there = pl.ds(pl.multiple_of((1 - mp) * half, half), half)
+    kv_ref[...] = (
+        mm(text_ref[:, here], near_ref[...]) + mm(text_ref[:, there], far_ref[...])
+    ).astype(bf16)
+    total_ref[...] = jnp.zeros(total_ref.shape, f32)
+    clear_edges(wide_grad, 0)
+    for tap in range(9):
+        flip_ref[(8 - tap) * C : (9 - tap) * C] = two_ref[tap * C : (tap + 1) * C].T
+    head_ref[...] = jnp.concatenate(
+        [heads_ref[...].astype(f32), jnp.zeros((8 - heads_ref.shape[0], C), f32)], axis=0
+    ).astype(bf16)
+    goal_ref[...] = jnp.zeros(goal_ref.shape, f32)
+    lane = lax.broadcasted_iota(jnp.int32, (tokens, C), 1)
+
+    def image(i, loss):
+        for k in range(3):
+            goal_ref[k : k + 1] = row_of(noise_ref[k], i)
+        both = kv_ref[pl.ds(pl.multiple_of(i * tokens, tokens), tokens), :]
+        zero = jnp.zeros((tokens, C), bf16)
+        low = lane < HEAD_DIM
+        key_ref[...] = jnp.concatenate(
+            [jnp.where(low, both[:, :C], zero), jnp.where(low, zero, both[:, :C])], axis=0
+        )
+        val_ref[...] = jnp.concatenate(
+            [jnp.where(low, both[:, C:], zero), jnp.where(low, zero, both[:, C:])], axis=0
+        )
+        dkey_ref[...] = jnp.zeros(dkey_ref.shape, f32)
+        dval_ref[...] = jnp.zeros(dval_ref.shape, f32)
+        mean_two, inv_two = stats_ref[i, 0:1], stats_ref[i, 1:2]
+        mean_three, inv_three = stats_ref[i, 2:3], stats_ref[i, 3:4]
+        gain, shift = stats_ref[i, 4:5], stats_ref[i, 5:6]
+        keep = lax.broadcasted_iota(jnp.int32, (CHUNK, tokens), 1) < lengths_ref[i]
+
+        def attend(j, carry):
+            total, moment, loss = carry
+            mid = mid_ref[i, span(j)]
+            hat = (mid - mean_three) * inv_three
+            query = (mm(hat.astype(bf16), query_ref[...]) * HEAD_DIM ** (-0.5)).astype(bf16)
+            scores = mm(query, key_ref[...], NT)
+            probs = []
+            for h in range(HEADS):
+                one = jnp.where(keep, scores[:, h * tokens : (h + 1) * tokens], -1e30)
+                one = jnp.exp(one - jnp.max(one, axis=1, keepdims=True))
+                probs.append(one / jnp.sum(one, axis=1, keepdims=True))
+            rounded = jnp.concatenate([p.astype(bf16) for p in probs], axis=1)
+            attended = mm(rounded, val_ref[...]).astype(bf16)
+            out = (mid + mm(attended, output_ref[...])).astype(bf16)
+            pred = mm(out, head_ref[...], NT)
+            error = pred - goal_ref[:, span(j)].T
+            loss = loss + fold(error * error)
+            dout = mm((2.0 * error).astype(bf16), head_ref[...]).astype(bf16)
+            dout_ref[span(j)] = dout
+            datt = mm(dout, output_ref[...], NT).astype(bf16)
+            dprobs = mm(datt, val_ref[...], NT).astype(bf16).astype(f32)
+            dval_ref[...] += mm(datt, rounded, TN)
+            dscores = []
+            for h in range(HEADS):
+                one = dprobs[:, h * tokens : (h + 1) * tokens]
+                inner = jnp.sum(one * probs[h], axis=1, keepdims=True)
+                dscores.append((probs[h] * (one - inner)).astype(bf16))
+            dscores = jnp.concatenate(dscores, axis=1)
+            dkey_ref[...] += mm(query, dscores, TN)
+            dquery = mm(dscores, key_ref[...]).astype(bf16)
+            dnorm = (mm(dquery, query_ref[...], NT) * HEAD_DIM ** (-0.5)).astype(bf16)
+            dnorm_ref[span(j)] = dnorm
+            dnorm = dnorm.astype(f32)
+            return (total + fold(dnorm), moment + fold(dnorm * hat), loss)
+
+        nothing = jnp.zeros((8, C), f32)
+        total, moment, loss = lax.fori_loop(0, CHUNKS, attend, (nothing, nothing, loss))
+        low_row = lax.broadcasted_iota(jnp.int32, (C, tokens), 0) < HEAD_DIM
+        cots = [
+            jnp.where(low_row, ref[:, :tokens], ref[:, tokens:]) for ref in (dkey_ref, dval_ref)
+        ]
+        cot_ref[:, pl.ds(pl.multiple_of(i * tokens, tokens), tokens)] = jnp.concatenate(
+            cots, axis=0
+        ).astype(bf16)
+        first, second = group_mean(total), group_mean(moment)
+
+        def middle(j, carry):
+            hat = (mid_ref[i, span(j)] - mean_three) * inv_three
+            grad = dout_ref[span(j)].astype(f32) + inv_three * (
+                dnorm_ref[span(j)].astype(f32) - first - hat * second
+            )
+            wide_grad[0, shifted(j, 1)] = spread(grad)
+            return carry
+
+        lax.fori_loop(0, CHUNKS, middle, 0)
+
+        def weights(which, source, grads):
+            grad_ref[...] = jnp.zeros(grad_ref.shape, f32)
+
+            def body(j, carry):
+                grad = grads(j)
+                for dy in range(3):
+                    grad_ref[:, dy * 3 * C : (dy + 1) * 3 * C] += mm(
+                        grad, source[i, shifted(j, dy)], TN
+                    )
+                return carry
+
+            lax.fori_loop(0, CHUNKS, body, 0)
+            total_ref[which] += grad_ref[...].astype(bf16).astype(f32)
+
+        weights(1, wide_two, lambda j: wide_grad[0, shifted(j, 1), C : 2 * C])
+
+        def inner(j, carry):
+            total, moment = carry
+            dact = conv_rows(wide_grad, 0, j, flip_ref).astype(bf16).astype(f32)
+            hat = (out_ref[i, span(j)] - mean_two) * inv_two
+            act = hat * gain + shift
+            gate = jax.nn.sigmoid(act)
+            dhat = dact * (gate * (1.0 + act * (1.0 - gate))) * gain
+            dhat_ref[span(j)] = dhat
+            return (total + fold(dhat), moment + fold(dhat * hat))
+
+        total, moment = lax.fori_loop(0, CHUNKS, inner, (nothing, nothing))
+        first, second = group_mean(total), group_mean(moment)
+
+        def early(j):
+            hat = (out_ref[i, span(j)] - mean_two) * inv_two
+            return (inv_two * (dhat_ref[span(j)] - first - hat * second)).astype(bf16)
+
+        weights(0, wide_one, early)
+        return loss
+
+    loss = lax.fori_loop(0, images, image, jnp.zeros((8, 8), f32))
+    loss_ref[...] = jnp.broadcast_to(
+        jnp.sum(jnp.sum(loss, axis=0, keepdims=True), axis=1, keepdims=True) / C, (1, C)
+    )
+    for which in range(2):
+        for block in range(9):
+            flat_ref[which, block * C : (block + 1) * C] = total_ref[
+                which, :, block * C : (block + 1) * C
+            ].T
+    flat_ref[:, 9 * C :] = jnp.zeros((2, 16, C), f32)
+    row = lax.broadcasted_iota(jnp.int32, (16, C), 0)
+
+    def owner(d, carry):
+        pieces = [
+            jnp.where(row < 9, flat_ref[which, pl.ds(d * 9, 16)], 0.0).astype(bf16)
+            for which in range(2)
+        ]
+        low = lax.rem(d, 2)
+        core = lax.rem(d // 2, 2)
+        y = lax.rem(d // 4, 4)
+        x = lax.rem(d // 16, 4)
+        high = d // 64
+        conv_ref[core, x, y, high * 2 + low] = jnp.concatenate(pieces, axis=1)
+        return carry
+
+    lax.fori_loop(0, 128, owner, 0)
+
+
+def backward(half, lengths, noise, text, near, far, made, conv_two, w_query, w_output, head):
+    images = noise.shape[1]
+    bf16, f32 = jnp.bfloat16, jnp.float32
+    tokens = text.shape[0] // images
+    vmem = pl.BlockSpec(memory_space=pltpu.VMEM)
+    smem = pl.BlockSpec(memory_space=pltpu.SMEM)
+    return pl.pallas_call(
+        backward_kernel,
+        out_shape=(
+            jax.ShapeDtypeStruct((2 * C, images * tokens), bf16),
+            jax.ShapeDtypeStruct((2, 4, 4, 4, 16, 2 * C), bf16),
+            jax.ShapeDtypeStruct((1, C), f32),
+        ),
+        in_specs=[smem] * 2 + [vmem] * 13,
+        out_specs=[vmem] * 3,
+        scratch_shapes=[
+            pltpu.VMEM((images * tokens, 2 * C), bf16),
+            pltpu.VMEM((2 * tokens, C), bf16),
+            pltpu.VMEM((2 * tokens, C), bf16),
+            pltpu.VMEM((C, 2 * tokens), f32),
+            pltpu.VMEM((C, 2 * tokens), f32),
+            pltpu.VMEM((PIXELS, C), bf16),
+            pltpu.VMEM((PIXELS, C), bf16),
+            pltpu.VMEM((PIXELS, C), f32),
+            pltpu.VMEM((1, PIXELS + 2 * EDGE, 3 * C), bf16),
+            pltpu.VMEM((C, 9 * C), f32),
+            pltpu.VMEM((2, 9 * C + 16, C), f32),
+            pltpu.VMEM((2, C, 9 * C), f32),
+            pltpu.VMEM((9 * C, C), bf16),
+            pltpu.VMEM((8, C), bf16),
+            pltpu.VMEM((8, PIXELS), f32),
+        ],
+        compiler_params=pltpu.CompilerParams(vmem_limit_bytes=LIMIT_B * 2**20),
+        cost_estimate=pl.CostEstimate(
+            flops=2 * 10**10, bytes_accessed=26 * 10**6, transcendentals=6 * 10**6
+        ),
+        name="backward",
+    )(half, lengths, noise, text, near, far, *made, conv_two, w_query, w_output, head)
+
+
+LIMIT_F = 8
+LIMIT_B = 20
 
 
 AXES = ("dp_0", "dp_1", "dp_2", "dp_3", "mp")
@@ -239,7 +549,7 @@
                 barrier, inc=1, device_id=axis_target(axis, to), device_id_type=MESH
             )
 
-    tokens = cot_ref.shape[0]
+    tokens = cot_ref.shape[1]
     for q in range(4):
         row = lax.broadcasted_iota(jnp.int32, (1024, 256), 0)
         col = lax.broadcasted_iota(jnp.int32, (1024, 256), 1)
@@ -254,7 +564,7 @@
         rows_ref[:, q * tokens : (q + 1) * tokens] = lax.dot_general(
             pick,
             cot_ref[...],
-            (((1,), (1,)), ((), ())),
+            (((1,), (0,)), ((), ())),
             preferred_element_type=jnp.float32,
         ).astype(jnp.bfloat16)
         for m in range(2):
@@ -452,19 +762,13 @@
             pltpu.SemaphoreType.DMA((10,)),
         ],
         compiler_params=pltpu.CompilerParams(
-            collective_id=0, has_side_effects=True, vmem_limit_bytes=40 * 2**20
+            collective_id=0, has_side_effects=True, vmem_limit_bytes=16 * 2**20
         ),
         cost_estimate=pl.CostEstimate(
             flops=3 * 10**9, bytes_accessed=8 * 10**6, transcendentals=0
         ),
         name="finish",
     )(text, cot, conv, loss)
-
-
-def by_owner(grad):
-    tiles = grad.reshape(2, 4, 4, 2, 2, 9, 128)
-    tiles = jnp.transpose(tiles, (3, 1, 2, 0, 4, 5, 6)).reshape(2, 4, 4, 4, 9, 128)
-    return jnp.pad(tiles, ((0, 0),) * 4 + ((0, 7), (0, 0))).astype(jnp.bfloat16)
 
 
 def local(
@@ -490,57 +794,34 @@
     features = text.shape[2]
     width = kv_weight.shape[1]
     half = kv_weight.shape[0]
-    piece = gather_directly(kv_weight, "mp", 0)
-    flat = jnp.dot(
-        text.reshape(images * tokens, piece.shape[0]), piece, preferred_element_type=jnp.float32
-    )
-    summed = flat.reshape(images, tokens, width)
-    keys_values = summed.astype(jnp.bfloat16)
-
-    def one_image(items):
-        clean_i, noise_i, low_i, aug_i, tstep, level, length, pairs = items
-        h_start, scale, shift = prepare(
-            clean_i, noise_i, low_i, aug_i, tstep, level, w_stem, w_time
-        )
-        keep = jnp.arange(tokens) < length
-        value, pullback = jax.vjp(
-            lambda first, second, third: image_loss(
-                first,
-                second,
-                third,
-                h_start,
-                scale,
-                shift,
-                keep,
-                w_query,
-                w_output,
-                w_head,
-                noise_i,
-            ),
-            conv_one,
-            conv_two,
-            pairs,
-        )
-        part_one, part_two, part_kv = pullback(jnp.ones((), jnp.float32))
-        return (part_one, part_two, part_kv, value)
-
-    parts_one, parts_two, parts_kv, values = lax.map(
-        one_image, (clean, noise, lowres, aug_noise, timesteps, aug_levels, lengths, keys_values)
-    )
-    local_one = jnp.sum(parts_one.astype(jnp.float32), axis=0)
-    local_two = jnp.sum(parts_two.astype(jnp.float32), axis=0)
-    local_loss = jnp.sum(values)
-    conv = jnp.concatenate([by_owner(local_one), by_owner(local_two)], axis=-1)
+    bf16, f32 = jnp.bfloat16, jnp.float32
+    far = lax.ppermute(kv_weight, "mp", [(0, 1), (1, 0)])
+
+    step, level = timesteps[:, None], aug_levels[:, None]
+    which = np.arange(4)
+    signal = signal_level(jnp.where(which < 2, step, level))
+    coefs = jnp.sqrt(jnp.where(which % 2 == 0, signal, 1.0 - signal))
+    lane = np.arange(4 * FREQS)
+    freqs = jnp.exp(-math.log(10000.0) * (lane % FREQS).astype(np.float32) / FREQS)
+    angles = jnp.where(lane < 2 * FREQS, step, level).astype(f32) * freqs
+    feature = jnp.where(lane % (2 * FREQS) < FREQS, jnp.sin(angles), jnp.cos(angles))
+    clean, noise, lowres, aug_noise = (
+        jnp.transpose(a, (1, 0, 2)) for a in (clean, noise, lowres, aug_noise)
+    )
+    made = forward(
+        coefs, clean, noise, lowres, aug_noise, w_stem, feature, w_time, conv_one, conv_two
+    )
+    mp = lax.axis_index("mp").astype(jnp.int32).reshape(1)
+    flat_text = text.reshape(images * tokens, features)
+    cot, conv, loss = backward(
+        mp, lengths, noise, flat_text, kv_weight, far, made, conv_two, w_query, w_output, w_head
+    )
     counts = (
         2 * half * width,
         conv_one.shape[0] * conv_one.shape[1],
-        images * lax.axis_size(DP_MP) * clean.shape[1] * clean.shape[2],
-    )
-    lane = lax.broadcasted_iota(jnp.int32, (1, 128), 1)
-    loss = jnp.where(lane == 0, local_loss, 0.0)
-    conv_one_update, conv_two_update, kv, mean = finish(
-        text.reshape(-1, features), parts_kv.reshape(-1, width), conv, loss, counts
-    )
+        images * lax.axis_size(DP_MP) * clean.shape[0] * clean.shape[2],
+    )
+    conv_one_update, conv_two_update, kv, mean = finish(flat_text, cot, conv, loss, counts)
     return (conv_one_update, conv_two_update, kv.T, mean[0, 0])
 
 

time: 284 us -> 141 us (0.50)
  matrix products: 94.6 us -> 0 us
  Pallas kernels: 38.3 us -> 126 us
  local copies, waits for them, and re-layouts: 63.9 us -> 8.98 us
  other arithmetic: 36 us -> 1.67 us
  waiting for transfers between devices: 25.4 us -> 0.01 us
  loops' own time: 15.4 us -> 0 us
    pallas_call x0 -> x2, Pallas kernels: none -> 87.2 us  [the longest x1 57.4 us: backward(): pl.pallas_call(backward_kernel, out_shape=(jax.ShapeDtypeStruct((2 * C, i...]
    dot_general x59 -> x0, matrix products: 55.6 us -> none  [the longest x4 12.4 us: image_loss(): jnp.einsum('kc,pc->kp', w_head, h_out.astype(jnp.bfloat16), preferred_ele...]
    conv_general_dilated x10 -> x0, matrix products: 39 us -> none  [convolve(): lax.conv_general_dilated(picture, kernel, (1, 1), 'SAME', dimension_numbe...]
    all_to_all x1 -> x0, waiting for transfers between devices: 25.4 us -> none  [from_everyone(): return lax.all_to_all(copies, axis, split_axis=0, concat_axis=0, tiled=True)]
    while x280 -> x0, local copies, waits for them, and re-layouts: 22.6 us -> none
    reduce_sum x27 -> x0, other arithmetic: 22.6 us -> none  [the longest x4 8.44 us: image_loss(): highest = jnp.max(scores, axis=1, keepdims=True)]
    another operation x1 -> x0, loops' own time: 15.4 us -> none  [local(): lax.map(one_image, (clean, noise, lowres, aug_noise, timesteps, aug_level...]
    dynamic_slice x14 -> x0, local copies, waits for them, and re-layouts: 12.6 us -> none  [local(): lax.map(one_image, (clean, noise, lowres, aug_noise, timesteps, aug_level...]
  transfers between devices with their start and end apart: 1 -> 1, of which waited for: 1 -> 0; matrix products, arithmetic and copies ran while one was open for 0% -> 1% of each run, Pallas kernels for 0% -> 21%
where the time goes in v2:
time: 141 us
  Pallas kernels  126 us (89%)
  local copies, waits for them, and re-layouts  8.98 us (6%)
  starting transfers between devices  2.11 us (1%)
  between operations  1.95 us (1%)
  other arithmetic  1.67 us (1%)
    pallas_call x1, Pallas kernels, backward(): pl.pallas_call(backward_kernel, out_shape=(jax.ShapeDtypeStruct((2 * C, i...  57.4 us
    pallas_call x1, Pallas kernels, finish(): pl.pallas_call(functools.partial(finish_kernel, counts), out_shape=(jax.S...  38.8 us
    pallas_call x1, Pallas kernels, forward(): pl.pallas_call(forward_kernel, out_shape=(flat, flat, wide, wide, jax.Sha...  29.8 us
    unnamed x35, local copies, waits for them, and re-layouts  8.98 us
  transfers between devices with their start and end apart: 1, of which 0 were waited for; matrix products, arithmetic and copies ran while one was open for 1% of the time, Pallas kernels for 21%

profile of v2, /device:TPU:0, one launch (start us, length us, event | category | flops | bytes accessed | tf_op | source)
XLA Modules:
  0.0 140.7 jit_solution(16267723480465046219)
XLA Ops:
  0.6 2.1 %collective-permute-start = (bf16[2048,256]{1,0:T(8,128)(2,1)}, bf16[2048,256]{1,0:T(8,128)(2,1)S(1)}, u32[]{:S(2)}, u32[]{:S(2)}) collective-permute-start(bf16[2048,256]{1,0:T(8,128)(2,1)} %near_ref.1), channel_id=1, source_target_pairs={{0,1},{1,0},{2,3},{3,2},{4,5},{5,4},{6,7},{7,6},{8,9},{9,8},{10,11... | collective-permute-start | bytes 3145736 | tf_op jit(solution)/shard_map/ppermute | solution.py:798
  2.7 0.8 cosine_select_fusion.feature_ref
  3.6 0.8 fusion.coef_ref
  4.4 0.0 copy-start.2
  4.4 1.0 copy-done.2
  5.4 0.0 copy-start.3
  5.4 1.0 copy-done.3
  6.4 0.0 copy-start.5
  6.4 0.9 copy-done.5
  7.3 0.0 copy-start.6
  7.3 0.9 copy-done.6
  8.2 0.0 copy-start.7
  8.2 0.9 copy-done.7
  9.1 0.0 copy-start.8
  9.1 0.9 copy-done.8
  10.0 0.0 copy-start.9
  10.0 0.9 copy-done.9
  10.9 0.0 copy-start.13
  10.9 0.7 copy-done.13
  11.6 0.0 copy-start
  11.6 0.0 copy-start.1
  11.6 0.0 copy-start.4
  11.6 0.0 copy-start.10
  11.6 0.0 copy-start.11
  11.6 0.0 copy-start.12
  11.6 0.0 copy-start.14
  11.6 0.0 copy-start.15
  11.6 29.8 %forward.1 = (f32[2,4096,128]{2,1,0:T(8,128)S(1)}, f32[2,4096,128]{2,1,0:T(8,128)S(1)}, bf16[2,4224,384]{2,1,0:T(8,128)(2,1)S(1)}, bf16[2,4224,384]{2,1,0:T(8,128)(2,1)S(1)}, f32[2,8,128]{2,1,0:T(8,128)S(1)}) custom-call(f32[2,4]{1,0:T(2,128)S(1)} %fusion.coef_ref, f32[3,2,4096]{2,1,0:T(2,128)S(1)} %bitcast.12, f32[3,2,4096]{2,1,0:T(2,128)S(1)} %bitcast.15, ...), custom_call_target="tpu_custom_call" | custom-call | flops 10000000000 | bytes 22000000 | tf_op jit(solution)/shard_map/forward/pallas_call | solution.py:215
  41.5 0.0 collective-permute-done.far_ref
  41.5 0.0 copy-done
  41.5 0.0 copy-done.1
  41.5 0.0 copy-done.4
  41.5 0.0 copy-done.10
  41.5 0.0 copy-done.11
  41.5 0.0 copy-done.12
  41.5 0.0 copy-done.14
  41.6 0.0 copy-done.15
  41.6 57.4 %backward.1 = (bf16[256,256]{1,0:T(8,128)(2,1)S(1)}, bf16[2,4,4,4,16,256]{5,4,3,2,1,0:T(8,128)(2,1)S(1)}, f32[1,128]{1,0:T(1,128)S(1)}) custom-call(s32[1]{0:T(128)} %bitcast.1.half_ref, s32[2]{0:T(128)S(1)} %copy-done.15, f32[3,2,4096]{2,1,0:T(2,128)S(1)} %bitcast.16, bf16[256,4096]{1,0:T(8,128)(2,1)S(1)} %bitcast.10, bf16[2048,256]{1,0:T(8,128)(2,1)S(1)} %copy-done.1, ...), custom_call_target="tpu_custom_call" | custom-call | flops 20000000000 | bytes 26000000 | tf_op jit(solution)/shard_map/backward/pallas_call | solution.py:443
  98.9 38.8 %finish.1 = (f32[9,128]{1,0:T(8,128)S(1)}, f32[9,128]{1,0:T(8,128)S(1)}, f32[4,2048]{1,0:T(4,128)S(1)}, f32[1,128]{1,0:T(1,128)S(1)}) custom-call(bf16[256,4096]{1,0:T(8,128)(2,1)S(1)} %bitcast.11, bf16[256,256]{1,0:T(8,128)(2,1)S(1)} %get-tuple-element.21.cot_ref, bf16[2,4,4,4,16,256]{5,4,3,2,1,0:T(8,128)(2,1)S(1)} %get-tuple-element.22.conv_ref, ...), custom_call_target="tpu_custom_call" | custom-call | flops 3000000000 | bytes 8000000 | tf_op jit(solution)/shard_map/finish/pallas_call | solution.py:735
  137.7 0.6 copy.29
  138.3 0.6 copy.30
  138.9 0.6 copy.31
Async XLA Ops:
  0.6 40.9 %collective-permute-start = (bf16[2048,256]{1,0:T(8,128)(2,1)}, bf16[2048,256]{1,0:T(8,128)(2,1)S(1)}, u32[]{:S(2)}, u32[]{:S(2)}) collective-permute-start(bf16[2048,256]{1,0:T(8,128)(2,1)} %near_ref.1), channel_id=1, source_target_pairs={{0,1},{1,0},{2,3},{3,2},{4,5},{5,4},{6,7},{7,6},{8,9},{9,8},{10,11... | collective-permute-start | bytes 3145736 | tf_op jit(solution)/shard_map/ppermute | solution.py:798
  4.4 1.0 copy-start.2
  5.4 1.0 copy-start.3
  6.4 0.9 copy-start.5
  7.3 0.9 copy-start.6
  8.2 0.9 copy-start.7
  9.1 0.9 copy-start.8
  10.0 0.9 copy-start.9
  10.9 0.7 copy-start.13
  11.6 29.9 %copy-start = (bf16[2,128,4096]{2,1,0:T(8,128)(2,1)S(1)}, bf16[2,128,4096]{2,1,0:T(8,128)(2,1)}, u32[]{:S(2)}) copy-start(bf16[2,128,4096]{2,1,0:T(8,128)(2,1)} %param.28) | copy-start | bytes 6291460
  11.6 29.9 %copy-start.1 = (bf16[2048,256]{1,0:T(8,128)(2,1)S(1)}, bf16[2048,256]{1,0:T(8,128)(2,1)}, u32[]{:S(2)}) copy-start(bf16[2048,256]{1,0:T(8,128)(2,1)} %near_ref.1) | copy-start | bytes 3145732
  11.6 29.9 %copy-start.4 = (bf16[1152,128]{1,0:T(8,128)(2,1)S(1)}, bf16[1152,128]{1,0:T(8,128)(2,1)}, u32[]{:S(2)}) copy-start(bf16[1152,128]{1,0:T(8,128)(2,1)} %two_ref.3) | copy-start | bytes 884740
  11.6 29.9 %copy-start.10 = (f32[2,3,4096]{2,0,1:T(2,128)S(1)}, f32[2,3,4096]{2,0,1:T(2,128)}, u32[]{:S(2)}) copy-start(f32[2,3,4096]{2,0,1:T(2,128)} %param.22) | copy-start | bytes 294916
  11.6 30.0 %copy-start.11 = (bf16[128,128]{1,0:T(8,128)(2,1)S(1)}, bf16[128,128]{1,0:T(8,128)(2,1)}, u32[]{:S(2)}) copy-start(bf16[128,128]{1,0:T(8,128)(2,1)} %query_ref.1) | copy-start | bytes 98308
  11.6 30.0 %copy-start.12 = (bf16[128,128]{1,0:T(8,128)(2,1)S(1)}, bf16[128,128]{1,0:T(8,128)(2,1)}, u32[]{:S(2)}) copy-start(bf16[128,128]{1,0:T(8,128)(2,1)} %output_ref.1) | copy-start | bytes 98308
  11.6 29.9 %copy-start.14 = (bf16[3,128]{1,0:T(4,128)(2,1)S(1)}, bf16[3,128]{1,0:T(4,128)(2,1)}, u32[]{:S(2)}) copy-start(bf16[3,128]{1,0:T(4,128)(2,1)} %heads_ref.1) | copy-start | bytes 2308
  11.6 29.9 %copy-start.15 = (s32[2]{0:T(128)S(1)}, s32[2]{0:T(128)}, u32[]{:S(2)}) copy-start(s32[2]{0:T(128)} %lengths_ref.1) | copy-start | bytes 28

commit v3 on v2

v3 whole, which is shorter than its diff:
```python
import functools
import math

import jax
import jax.numpy as jnp
import numpy as np
from jax import lax
from jax.sharding import Mesh
from jax.sharding import PartitionSpec as P
from jax.experimental import pallas as pl
from jax.experimental.pallas import tpu as pltpu

S = 64
GROUPS = 32
HEADS = 2
HEAD_DIM = 64
FREQS = 64
STEPS = 1000
DP_MP = ("dp_0", "dp_1", "dp_2", "dp_3", "mp")
DP = ("dp_0", "dp_1", "dp_2", "dp_3")


def signal_level(index):
    ratio = (index.astype(jnp.float32) / STEPS + 0.008) / 1.008
    cosine = jnp.cos(ratio * (math.pi / 2.0))
    return cosine * cosine


PIXELS = S * S
CHUNK = 512
CHUNKS = PIXELS // CHUNK
EDGE = S
C = 128


def group_total(line):
    lane = lax.broadcasted_iota(jnp.int32, line.shape, 1)
    pair = line + jnp.where(
        lane % 2 == 0, pltpu.roll(line, C - 1, 1), pltpu.roll(line, 1, 1)
    )
    return pair + jnp.where(
        lane % 4 < 2, pltpu.roll(pair, C - 2, 1), pltpu.roll(pair, 2, 1)
    )


def group_mean(total):
    line = jnp.broadcast_to(jnp.sum(total, axis=0, keepdims=True), (8, C)) / PIXELS
    return group_total(line)[0:1] / (C // GROUPS)


def row_of(value, i):
    row = value[0:1]
    for r in range(1, value.shape[0]):
        row = jnp.where(i == r, value[r : r + 1], row)
    return row


def fold(value):
    return jnp.sum(value.reshape(-1, 8, value.shape[-1]), axis=0)


def spread(act):
    column = lax.broadcasted_iota(jnp.int32, act.shape, 0) % S
    rows = act.shape[0]
    left = jnp.where(column == 0, 0.0, pltpu.roll(act, 1, 0))
    right = jnp.where(column == S - 1, 0.0, pltpu.roll(act, rows - 1, 0))
    return jnp.concatenate(
        [left.astype(jnp.bfloat16), act.astype(jnp.bfloat16), right.astype(jnp.bfloat16)], axis=1
    )


def span(j, size=CHUNK):
    return pl.ds(pl.multiple_of(j * size, size), size)


LINES = CHUNK // S


def inside(j, shift=1):
    return pl.ds(j * LINES + shift, LINES)


def clear_edges(ref, i):
    zero = jnp.zeros((S, ref.shape[-1]), jnp.bfloat16)
    ref[i, 0] = zero
    ref[i, S + 1] = zero


CONV = 2048
PAIRS = CONV // (2 * S)


def fill_pairs(pair_ref, block_of):
    for iy in range(4):
        for dx in range(3):
            at = (iy * 3 + dx) * C
            for oy in range(2):
                dy = iy - oy
                block = (
                    block_of(dy * 3 + dx) if 0 <= dy < 3 else jnp.zeros((C, C), jnp.bfloat16)
                )
                pair_ref[at : at + C, oy * C : (oy + 1) * C] = block


def conv_rows(wide_ref, i, j, pair_ref):
    rows = [
        jnp.concatenate([wide_ref[i, 2 * (j * PAIRS + t) + iy] for iy in range(4)], axis=1)
        for t in range(PAIRS)
    ]
    value = jnp.dot(
        jnp.concatenate(rows, axis=0), pair_ref[...], preferred_element_type=jnp.float32
    )
    lines = []
    for t in range(PAIRS):
        for oy in range(2):
            lines.append(value[t * S : (t + 1) * S, oy * C : (oy + 1) * C])
    return jnp.concatenate(lines, axis=0)


def loop_sum(body, size=CHUNK):
    return lax.fori_loop(0, PIXELS // size, body, jnp.zeros((8, C), jnp.float32))


def forward_kernel(
    coef_ref,
    feature_ref,
    clean_in,
    noise_in,
    low_in,
    aug_in,
    stem_in,
    time_in,
    one_in,
    two_in,
    mid_ref,
    out_ref,
    wide_one,
    wide_two,
    stats_ref,
    clean_ref,
    noise_ref,
    low_ref,
    aug_ref,
    stem_ref,
    time_ref,
    one_ref,
    two_ref,
    planes_ref,
    stems_ref,
    embed_ref,
    lhs_ref,
    pair_one,
    pair_two,
    sems,
):
    sources = (stem_in, time_in, clean_in, noise_in, low_in, aug_in, one_in, two_in)
    targets = (stem_ref, time_ref, clean_ref, noise_ref, low_ref, aug_ref, one_ref, two_ref)
    copies = [
        pltpu.make_async_copy(sources[n], targets[n], sems.at[n]) for n in range(len(sources))
    ]
    for copy in copies:
        copy.start()
    images = clean_ref.shape[1]
    for copy in copies:
        copy.wait()
    fill_pairs(pair_one, lambda tap: one_ref[tap * C : (tap + 1) * C])
    fill_pairs(pair_two, lambda tap: two_ref[tap * C : (tap + 1) * C])
    w = jnp.concatenate([stem_ref[...], jnp.zeros((2, C), jnp.float32)], axis=0)
    w1 = w.astype(jnp.bfloat16).astype(jnp.float32)
    w2 = (w - w1).astype(jnp.bfloat16).astype(jnp.float32)
    w3 = w - w1 - w2
    stems_ref[...] = jnp.concatenate([w1, w2, w1, w3, w2, w1], axis=0).astype(jnp.bfloat16)
    feature = jnp.concatenate(
        [feature_ref[...], jnp.zeros((8 - images, 2 * C), jnp.float32)], axis=0
    )
    embed = jnp.dot(
        feature,
        time_ref[...],
        precision=lax.Precision.HIGHEST,
        preferred_element_type=jnp.float32,
    )
    embed_ref[...] = embed * jax.nn.sigmoid(embed)
    planes_ref[...] = jnp.zeros(planes_ref.shape, jnp.float32)

    def image(i, carry):
        for k in range(3):
            planes_ref[k : k + 1] = (
                coef_ref[i, 0] * row_of(clean_ref[k], i)
                + coef_ref[i, 1] * row_of(noise_ref[k], i)
            )
            planes_ref[3 + k : 4 + k] = (
                coef_ref[i, 2] * row_of(low_ref[k], i) + coef_ref[i, 3] * row_of(aug_ref[k], i)
            )
        s = planes_ref[...]
        s1 = s.astype(jnp.bfloat16).astype(jnp.float32)
        s2 = (s - s1).astype(jnp.bfloat16).astype(jnp.float32)
        s3 = s - s1 - s2
        lhs_ref[...] = jnp.concatenate([s1, s1, s2, s1, s2, s3], axis=0).astype(jnp.bfloat16)
        clear_edges(wide_one, i)
        clear_edges(wide_two, i)

        def stem(j, total):
            h = lax.dot_general(
                lhs_ref[:, span(j)],
                stems_ref[...],
                (((0,), (0,)), ((), ())),
                preferred_element_type=jnp.float32,
            )
            mid_ref[i, span(j)] = h
            return total + fold(h)

        def variance(ref, mean):
            def body(j, total):
                centred = ref[i, span(j)] - mean
                return total + fold(centred * centred)

            return lax.rsqrt(group_mean(loop_sum(body)) + 1e-05)

        mean_one = group_mean(loop_sum(stem))
        inv_one = variance(mid_ref, mean_one)

        def first(j, carry):
            act = (mid_ref[i, span(j)] - mean_one) * inv_one
            wide_one[i, inside(j)] = spread(act * jax.nn.sigmoid(act)).reshape(LINES, S, 3 * C)
            return carry

        lax.fori_loop(0, CHUNKS, first, 0)

        def conv_first(j, total):
            value = conv_rows(wide_one, i, j, pair_one)
            out_ref[i, span(j, CONV)] = value
            return total + fold(value)

        mean_two = group_mean(loop_sum(conv_first, CONV))
        inv_two = variance(out_ref, mean_two)
        gain = 1.0 + row_of(embed_ref[0:images, 0:C], i)
        shift = row_of(embed_ref[0:images, C : 2 * C], i)

        def next_act(j, carry):
            act = (out_ref[i, span(j)] - mean_two) * inv_two * gain + shift
            wide_two[i, inside(j)] = spread(act * jax.nn.sigmoid(act)).reshape(LINES, S, 3 * C)
            return carry

        lax.fori_loop(0, CHUNKS, next_act, 0)

        def conv_second(j, total):
            value = mid_ref[i, span(j, CONV)] + conv_rows(wide_two, i, j, pair_two)
            mid_ref[i, span(j, CONV)] = value
            return total + fold(value)

        mean_three = group_mean(loop_sum(conv_second, CONV))
        inv_three = variance(mid_ref, mean_three)
        stats_ref[i] = jnp.concatenate(
            [mean_two, inv_two, mean_three, inv_three, gain, shift, gain, shift], axis=0
        )
        return carry

    lax.fori_loop(0, images, image, 0)


def forward(coefs, feature, *arrays):
    images = feature.shape[0]
    bf16, f32 = jnp.bfloat16, jnp.float32
    wide = jax.ShapeDtypeStruct((images, S + 2, S, 3 * C), bf16)
    flat = jax.ShapeDtypeStruct((images, PIXELS, C), f32)
    return pl.pallas_call(
        forward_kernel,
        out_shape=(flat, flat, wide, wide, jax.ShapeDtypeStruct((images, 8, C), f32)),
        in_specs=[
            pl.BlockSpec(memory_space=pltpu.SMEM),
            pl.BlockSpec(memory_space=pltpu.VMEM),
        ]
        + [pl.BlockSpec(memory_space=pltpu.HBM)] * 8,
        out_specs=[pl.BlockSpec(memory_space=pltpu.VMEM)] * 5,
        scratch_shapes=[pltpu.VMEM(a.shape, a.dtype) for a in arrays]
        + [
            pltpu.VMEM((8, PIXELS), f32),
            pltpu.VMEM((48, C), bf16),
            pltpu.VMEM((8, 2 * C), f32),
            pltpu.VMEM((48, PIXELS), bf16),
            pltpu.VMEM((12 * C, 2 * C), bf16),
            pltpu.VMEM((12 * C, 2 * C), bf16),
            pltpu.SemaphoreType.DMA((8,)),
        ],
        compiler_params=pltpu.CompilerParams(vmem_limit_bytes=LIMIT_F * 2**20),
        cost_estimate=pl.CostEstimate(
            flops=10**10, bytes_accessed=22 * 10**6, transcendentals=2 * 10**6
        ),
        name="forward",
    )(coefs, feature, *arrays)


TN = (((0,), (0,)), ((), ()))
NT = (((1,), (1,)), ((), ()))


def mm(a, b, dims=(((1,), (0,)), ((), ()))):
    return lax.dot_general(a, b, dims, preferred_element_type=jnp.float32)


def attend_kernel(
    half_ref,
    lengths_ref,
    noise_ref,
    text_ref,
    near_ref,
    far_ref,
    mid_ref,
    stats_ref,
    query_ref,
    output_ref,
    heads_ref,
    cot_ref,
    wide_grad,
    loss_ref,
    kv_ref,
    key_ref,
    val_ref,
    dkey_ref,
    dval_ref,
    dnorm_ref,
    dout_ref,
    head_ref,
    goal_ref,
):
    bf16, f32 = jnp.bfloat16, jnp.float32
    images = noise_ref.shape[1]
    tokens = text_ref.shape[0] // images
    half = near_ref.shape[0]
    mp = half_ref[0]
    here = pl.ds(pl.multiple_of(mp * half, half), half)
    there = pl.ds(pl.multiple_of((1 - mp) * half, half), half)
    kv_ref[...] = (
        mm(text_ref[:, here], near_ref[...]) + mm(text_ref[:, there], far_ref[...])
    ).astype(bf16)
    head_ref[...] = jnp.concatenate(
        [heads_ref[...].astype(f32), jnp.zeros((8 - heads_ref.shape[0], C), f32)], axis=0
    ).astype(bf16)
    goal_ref[...] = jnp.zeros(goal_ref.shape, f32)
    lane = lax.broadcasted_iota(jnp.int32, (tokens, C), 1)
    nothing = jnp.zeros((8, C), f32)

    def image(i, loss):
        clear_edges(wide_grad, i)
        for k in range(3):
            goal_ref[k : k + 1] = row_of(noise_ref[k], i)
        both = kv_ref[pl.ds(pl.multiple_of(i * tokens, tokens), tokens), :]
        zero = jnp.zeros((tokens, C), bf16)
        low = lane < HEAD_DIM
        key_ref[...] = jnp.concatenate(
            [jnp.where(low, both[:, :C], zero), jnp.where(low, zero, both[:, :C])], axis=0
        )
        val_ref[...] = jnp.concatenate(
            [jnp.where(low, both[:, C:], zero), jnp.where(low, zero, both[:, C:])], axis=0
        )
        dkey_ref[...] = jnp.zeros(dkey_ref.shape, f32)
        dval_ref[...] = jnp.zeros(dval_ref.shape, f32)
        mean_three, inv_three = stats_ref[i, 2:3], stats_ref[i, 3:4]
        keep = lax.broadcasted_iota(jnp.int32, (ATTEND, tokens), 1) < lengths_ref[i]

        def attend(j, carry):
            total, moment, loss = carry
            mid = mid_ref[i, span(j, ATTEND)]
            hat = (mid - mean_three) * inv_three
            query = (mm(hat.astype(bf16), query_ref[...]) * HEAD_DIM ** (-0.5)).astype(bf16)
            scores = mm(query, key_ref[...], NT)
            probs = []
            for h in range(HEADS):
                one = jnp.where(keep, scores[:, h * tokens : (h + 1) * tokens], -1e30)
                one = jnp.exp(one - jnp.max(one, axis=1, keepdims=True))
                probs.append(one / jnp.sum(one, axis=1, keepdims=True))
            rounded = jnp.concatenate([p.astype(bf16) for p in probs], axis=1)
            attended = mm(rounded, val_ref[...]).astype(bf16)
            out = (mid + mm(attended, output_ref[...])).astype(bf16)
            pred = mm(out, head_ref[...], NT)
            error = pred - goal_ref[:, span(j, ATTEND)].T
            loss = loss + fold(error * error)
            dout = mm((2.0 * error).astype(bf16), head_ref[...]).astype(bf16)
            dout_ref[span(j, ATTEND)] = dout
            datt = mm(dout, output_ref[...], NT).astype(bf16)
            dprobs = mm(datt, val_ref[...], NT).astype(bf16).astype(f32)
            dval_ref[...] += mm(datt, rounded, TN)
            dscores = []
            for h in range(HEADS):
                one = dprobs[:, h * tokens : (h + 1) * tokens]
                inner = jnp.sum(one * probs[h], axis=1, keepdims=True)
                dscores.append((probs[h] * (one - inner)).astype(bf16))
            dscores = jnp.concatenate(dscores, axis=1)
            dkey_ref[...] += mm(query, dscores, TN)
            dquery = mm(dscores, key_ref[...]).astype(bf16)
            dnorm = (mm(dquery, query_ref[...], NT) * HEAD_DIM ** (-0.5)).astype(bf16)
            dnorm_ref[span(j, ATTEND)] = dnorm
            dnorm = dnorm.astype(f32)
            return (total + fold(dnorm), moment + fold(dnorm * hat), loss)

        total, moment, loss = lax.fori_loop(0, PIXELS // ATTEND, attend, (nothing, nothing, loss))
        low_row = lax.broadcasted_iota(jnp.int32, (C, tokens), 0) < HEAD_DIM
        cots = [
            jnp.where(low_row, ref[:, :tokens], ref[:, tokens:]) for ref in (dkey_ref, dval_ref)
        ]
        cot_ref[:, pl.ds(pl.multiple_of(i * tokens, tokens), tokens)] = jnp.concatenate(
            cots, axis=0
        ).astype(bf16)
        first, second = group_mean(total), group_mean(moment)

        def middle(j, carry):
            hat = (mid_ref[i, span(j)] - mean_three) * inv_three
            grad = dout_ref[span(j)].astype(f32) + inv_three * (
                dnorm_ref[span(j)].astype(f32) - first - hat * second
            )
            wide_grad[i, inside(j)] = spread(grad).reshape(LINES, S, 3 * C)
            return carry

        lax.fori_loop(0, CHUNKS, middle, 0)

        return loss

    loss = lax.fori_loop(0, images, image, jnp.zeros((8, 8), f32))
    loss_ref[...] = jnp.broadcast_to(
        jnp.sum(jnp.sum(loss, axis=0, keepdims=True), axis=1, keepdims=True) / C, (1, C)
    )


def attention(half, lengths, noise, text, near, far, mid, stats, w_query, w_output, head):
    images = noise.shape[1]
    bf16, f32 = jnp.bfloat16, jnp.float32
    tokens = text.shape[0] // images
    vmem = pl.BlockSpec(memory_space=pltpu.VMEM)
    smem = pl.BlockSpec(memory_space=pltpu.SMEM)
    return pl.pallas_call(
        attend_kernel,
        out_shape=(
            jax.ShapeDtypeStruct((2 * C, images * tokens), bf16),
            jax.ShapeDtypeStruct((images, S + 2, S, 3 * C), bf16),
            jax.ShapeDtypeStruct((1, C), f32),
        ),
        in_specs=[smem] * 2 + [vmem] * 9,
        out_specs=[vmem] * 3,
        scratch_shapes=[
            pltpu.VMEM((images * tokens, 2 * C), bf16),
            pltpu.VMEM((2 * tokens, C), bf16),
            pltpu.VMEM((2 * tokens, C), bf16),
            pltpu.VMEM((C, 2 * tokens), f32),
            pltpu.VMEM((C, 2 * tokens), f32),
            pltpu.VMEM((PIXELS, C), bf16),
            pltpu.VMEM((PIXELS, C), bf16),
            pltpu.VMEM((8, C), bf16),
            pltpu.VMEM((8, PIXELS), f32),
        ],
        compiler_params=pltpu.CompilerParams(vmem_limit_bytes=LIMIT_A * 2**20),
        cost_estimate=pl.CostEstimate(
            flops=10**10, bytes_accessed=16 * 10**6, transcendentals=6 * 10**6
        ),
        name="attention",
    )(half, lengths, noise, text, near, far, mid, stats, w_query, w_output, head)


ATTEND = 1024
LIMIT_F = 12
LIMIT_A = 16
LIMIT_T = 20


MESH = pl.DeviceIdType.MESH
LINE = 4
WIDTHS = (256, 256, 128, 128)
ORDERS = (("x", "y", "z"), ("y", "z", "x"), ("z", "x", "y"), ("z", "x", "y"))
COLUMNS = (0, 256, 640, 512)


def axis_target(axis, to):
    if axis == "x":
        return {"dp_1": to}
    if axis == "y":
        return {"dp_2": to}
    if axis == "z":
        return {"dp_0": to // 2, "mp": lax.rem(to, 2)}
    return {"dp_3": to}


def remote(source, target, send, recv, axis, to):
    copy = pltpu.make_async_remote_copy(
        src_ref=source,
        dst_ref=target,
        send_sem=send,
        recv_sem=recv,
        device_id=axis_target(axis, to),
        device_id_type=MESH,
    )
    copy.start()
    return copy


def finish_kernel(
    counts,
    text_ref,
    cot_ref,
    loss_ref,
    out_ref,
    wide_one,
    wide_two,
    wide_grad,
    stats_ref,
    two_ref,
    one_out,
    two_out,
    kv_out,
    mean_out,
    rows_ref,
    dhat_ref,
    grad_ref,
    flat_ref,
    sum_ref,
    flip_ref,
    grad_pad,
    total_ref,
    slots,
    send_sems,
    recv_sems,
    slot_send,
    slot_recv,
    *stages,
):
    bf16, f32 = jnp.bfloat16, jnp.float32
    images = stats_ref.shape[0]
    own, core_in, held, line_in, second, second_in, third, third_in = (
        stages[n * 4 : (n + 1) * 4] for n in range(8)
    )
    place = {
        "x": lax.axis_index("dp_1"),
        "y": lax.axis_index("dp_2"),
        "z": lax.axis_index("dp_0") * 2 + lax.axis_index("mp"),
        "core": lax.axis_index("dp_3"),
    }
    core = place["core"]
    other = 1 - core
    barrier = pltpu.get_barrier_semaphore()
    for outer, inner, size in (("z", "core", 2), ("x", "y", LINE)):
        for k in range(1, LINE * size):
            to = {
                **axis_target(outer, lax.rem(place[outer] + k // size, LINE)),
                **axis_target(inner, lax.rem(place[inner] + k % size, size)),
            }
            pl.semaphore_signal(barrier, inc=1, device_id=to, device_id_type=MESH)

    sent = []

    def start_core(c):
        copy = remote(
            own[c].at[other],
            core_in[c],
            send_sems.at[c * 10],
            recv_sems.at[c * 10],
            "core",
            other,
        )
        sent.append(copy)
        return [copy]

    def part_of(left, axis, at):
        return tuple(at if name == axis else slice(None) for name in left)

    def exchange(c, stage, source, left, into):
        axis = ORDERS[c][stage]
        started = []
        for k in range(1, LINE):
            to = lax.rem(place[axis] + k, LINE)
            slot = c * 10 + stage * 3 + k
            started.append(
                remote(
                    source[c].at[part_of(left, axis, to)],
                    into[c].at[k - 1],
                    send_sems.at[slot],
                    recv_sems.at[slot],
                    axis,
                    to,
                )
            )
        sent.extend(started)
        return started

    def arrive(copies):
        for copy in copies:
            copy.wait_recv()

    def to_first(c, copies):
        arrive(copies)

        def add(i, carry):
            held[c][i] = (own[c][core, i].astype(f32) + core_in[c][i].astype(f32)).astype(bf16)
            return carry

        lax.fori_loop(0, LINE, add, 0)
        return exchange(c, 0, held, ("x", "y", "z"), line_in)

    def to_second(c, copies):
        arrive(copies)
        axis = ORDERS[c][0]
        rest = [name for name in ("x", "y", "z") if name != axis]
        for i in range(LINE):
            index = tuple(
                place[axis] if name == axis else (i if name == rest[0] else slice(None))
                for name in ("x", "y", "z")
            )
            value = held[c][index].astype(f32)
            for k in range(LINE - 1):
                value = value + line_in[c][k, i].astype(f32)
            second[c][i] = value.astype(bf16)
        return exchange(c, 1, second, tuple(rest), second_in)

    def to_third(c, copies):
        arrive(copies)
        left = tuple(name for name in ("x", "y", "z") if name != ORDERS[c][0])
        axis = ORDERS[c][1]
        value = second[c][part_of(left, axis, place[axis])].astype(f32)
        for k in range(LINE - 1):
            value = value + second_in[c][k].astype(f32)
        third[c][...] = value.astype(bf16)
        return exchange(c, 2, third, (ORDERS[c][2],), third_in)

    def to_total(c, copies):
        arrive(copies)
        value = third[c][place[ORDERS[c][2]]].astype(f32)
        for k in range(LINE - 1):
            value = value + third_in[c][k].astype(f32)
        total_ref[:, COLUMNS[c] : COLUMNS[c] + WIDTHS[c]] = value

    tokens = cot_ref.shape[1]
    row = lax.broadcasted_iota(jnp.int32, (1024, 256), 0)
    col = lax.broadcasted_iota(jnp.int32, (1024, 256), 1)
    owner = ((row // 16) % 2 * 32 + row // 32 % 16 * 2 + row // 512) * 4 + row % 4
    pick = jnp.where(owner == col, 1.0, 0.0).astype(bf16)
    picked = mm(pick, cot_ref[...])
    quarter = (row // 4) % 4
    for q in range(4):
        rows_ref[:, q * tokens : (q + 1) * tokens] = jnp.where(
            quarter[:, :tokens] == q, picked, 0.0
        ).astype(bf16)

    def block(m, carry):
        for c in range(2):
            at = m * 2048 + c * 256
            wide = jnp.concatenate(
                [
                    text_ref[:, pl.ds(pl.multiple_of(at + q * 512, 256), 256)]
                    for q in range(4)
                ],
                axis=0,
            )
            for half in range(2):
                value = mm(rows_ref[half * 512 : (half + 1) * 512, :], wide).astype(bf16)
                value = value.reshape(4, 4, 2, 16, 256)
                for zh in range(2):
                    own[c][half, :, :, zh * 2 + m] = value[:, :, zh]
        return carry

    lax.fori_loop(0, 2, block, 0)
    pl.semaphore_wait(barrier, 22)
    first_kv = [start_core(0), start_core(1)]

    fill_pairs(flip_ref, lambda tap: two_ref[(8 - tap) * C : (9 - tap) * C].T)
    clear_edges(grad_pad, 0)
    sum_ref[...] = jnp.zeros(sum_ref.shape, f32)
    flat_ref[:, 9 * C :] = jnp.zeros((2, 16, C), f32)
    nothing = jnp.zeros((8, C), f32)

    def weights(which, i, source, grad_of):
        grad_ref[...] = jnp.zeros(grad_ref.shape, f32)

        def body(j, carry):
            grads = [grad_of(inside(j, 2 - dy)).reshape(CHUNK, C) for dy in range(3)]
            grad_ref[...] += mm(
                jnp.concatenate(grads, axis=1), source[i, inside(j)].reshape(CHUNK, 3 * C), TN
            )
            return carry

        lax.fori_loop(0, CHUNKS, body, 0)
        sum_ref[which] += grad_ref[...].astype(bf16).astype(f32)

    def pack(which, c):
        for dy in range(3):
            for dx in range(3):
                at = (dy * 3 + dx) * C
                flat_ref[which, at : at + C] = sum_ref[
                    which, dy * C : (dy + 1) * C, dx * C : (dx + 1) * C
                ].T
        row = lax.broadcasted_iota(jnp.int32, (16, C), 0)

        for d in range(128):
            piece = jnp.where(row < 9, flat_ref[which, d * 9 : d * 9 + 16], 0.0).astype(bf16)
            own[c][d // 2 % 2, d // 16 % 4, d // 4 % 4, d // 64 * 2 + d % 2] = piece

    def act_grad(i):
        mean_two, inv_two = stats_ref[i, 0:1], stats_ref[i, 1:2]
        gain, shift = stats_ref[i, 4:5], stats_ref[i, 5:6]

        def inner(j, carry):
            total, moment = carry
            dact = conv_rows(wide_grad, i, j, flip_ref).astype(bf16).astype(f32)
            at = span(j, CONV)
            hat = (out_ref[i, at] - mean_two) * inv_two
            act = hat * gain + shift
            gate = jax.nn.sigmoid(act)
            dhat = dact * (gate * (1.0 + act * (1.0 - gate))) * gain
            dhat_ref[at] = dhat
            return (total + fold(dhat), moment + fold(dhat * hat))

        total, moment = lax.fori_loop(0, PIXELS // CONV, inner, (nothing, nothing))
        return mean_two, inv_two, group_mean(total), group_mean(moment)

    def early_grad(i, lines):
        mean_two, inv_two, first, moment = lines

        def early(j, carry):
            hat = (out_ref[i, span(j)] - mean_two) * inv_two
            grad = inv_two * (dhat_ref[span(j)] - first - hat * moment)
            grad_pad[0, inside(j)] = grad.astype(bf16).reshape(LINES, S, C)
            return carry

        lax.fori_loop(0, CHUNKS, early, 0)
        weights(0, i, wide_one, lambda at: grad_pad[0, at])

    for i in range(images):
        weights(1, i, wide_two, lambda at, i=i: wide_grad[i, at, :, C : 2 * C])
    copies = [to_first(0, first_kv[0]), to_first(1, first_kv[1])]
    pack(1, 2)
    copies.append(start_core(2))
    lines = act_grad(0)
    copies[2] = to_first(2, copies[2])
    early_grad(0, lines)
    for c in range(2):
        copies[c] = to_second(c, copies[c])
    lines = act_grad(1)
    copies[2] = to_second(2, copies[2])
    for c in range(2):
        copies[c] = to_third(c, copies[c])
    early_grad(1, lines)
    pack(0, 3)
    copies.append(start_core(3))
    copies[2] = to_third(2, copies[2])
    for c in range(2):
        to_total(c, copies[c])
    copies[3] = to_first(3, copies[3])
    to_total(2, copies[2])
    copies[3] = to_second(3, copies[3])
    copies[3] = to_third(3, copies[3])
    to_total(3, copies[3])

    value = total_ref[...]
    square = value * value
    kv_line = jnp.sum(square[:, :512], axis=0, keepdims=True)
    kv_line = (
        kv_line[:, :128] + kv_line[:, 128:256] + kv_line[:, 256:384] + kv_line[:, 384:512]
    )
    conv_line = jnp.sum(square[:, 512:], axis=0, keepdims=True)
    row = lax.broadcasted_iota(jnp.int32, (8, 128), 0)
    tile = jnp.where(row == 0, kv_line, 0.0)
    tile = jnp.where(row == 1, conv_line[:, :128], tile)
    tile = jnp.where(row == 2, conv_line[:, 128:], tile)
    tile = jnp.where(row == 3, loss_ref[...], tile)
    at = 0
    for stage, (outer, inner) in enumerate((("z", "core"), ("x", "y"))):
        sizes = (LINE, 2 if inner == "core" else LINE)
        mine = place[outer] * sizes[1] + place[inner]
        slots[stage, mine] = tile
        started = []
        for k in range(1, sizes[0] * sizes[1]):
            to = {
                **axis_target(outer, lax.rem(place[outer] + k // sizes[1], LINE)),
                **axis_target(inner, lax.rem(place[inner] + k % sizes[1], sizes[1])),
            }
            copy = pltpu.make_async_remote_copy(
                src_ref=slots.at[stage, mine],
                dst_ref=slots.at[stage, mine],
                send_sem=slot_send.at[at],
                recv_sem=slot_recv.at[at],
                device_id=to,
                device_id_type=MESH,
            )
            copy.start()
            started.append(copy)
            at += 1
        arrive(started)
        sent.extend(started)
        tile = slots[stage, 0]
        for k in range(1, sizes[0] * sizes[1]):
            tile = tile + slots[stage, k]
    sums = jnp.sum(tile, axis=1, keepdims=True)
    kv_scale = lax.rsqrt(sums[0:1] / counts[0] + 1e-06)
    one_scale = lax.rsqrt(sums[1:2] / counts[1] + 1e-06)
    two_scale = lax.rsqrt(sums[2:3] / counts[1] + 1e-06)
    one_out[...] = total_ref[0:9, 512:640] * one_scale
    two_out[...] = total_ref[0:9, 640:768] * two_scale
    for q in range(4):
        kv_out[:, q * 512 : (q + 1) * 512] = total_ref[q * 4 : (q + 1) * 4, 0:512] * kv_scale
    mean_out[...] = jnp.broadcast_to(sums[3:4] / counts[2], mean_out.shape)
    for copy in sent:
        copy.wait_send()


def finish(counts, *arrays):
    bf16, f32 = jnp.bfloat16, jnp.float32
    vmem = pl.BlockSpec(memory_space=pltpu.VMEM)
    stages = [
        (2, 4, 4, 4, 16),
        (4, 4, 4, 16),
        (4, 4, 4, 16),
        (3, 4, 4, 16),
        (4, 4, 16),
        (3, 4, 16),
        (4, 16),
        (3, 16),
    ]
    return pl.pallas_call(
        functools.partial(finish_kernel, counts),
        out_shape=(
            jax.ShapeDtypeStruct((9, 128), f32),
            jax.ShapeDtypeStruct((9, 128), f32),
            jax.ShapeDtypeStruct((4, 2048), f32),
            jax.ShapeDtypeStruct((1, 128), f32),
        ),
        in_specs=[vmem] * len(arrays),
        out_specs=[vmem] * 4,
        scratch_shapes=[
            pltpu.VMEM((1024, 1024), bf16),
            pltpu.VMEM((PIXELS, C), f32),
            pltpu.VMEM((3 * C, 3 * C), f32),
            pltpu.VMEM((2, 9 * C + 16, C), f32),
            pltpu.VMEM((2, 3 * C, 3 * C), f32),
            pltpu.VMEM((12 * C, 2 * C), bf16),
            pltpu.VMEM((1, S + 2, S, C), bf16),
            pltpu.VMEM((16, 768), f32),
            pltpu.VMEM((2, 16, 8, 128), f32),
            pltpu.SemaphoreType.DMA((40,)),
            pltpu.SemaphoreType.DMA((40,)),
            pltpu.SemaphoreType.DMA((22,)),
            pltpu.SemaphoreType.DMA((22,)),
        ]
        + [pltpu.VMEM((*shape, width), bf16) for shape in stages for width in WIDTHS],
        compiler_params=pltpu.CompilerParams(
            collective_id=0, has_side_effects=True, vmem_limit_bytes=LIMIT_T * 2**20
        ),
        cost_estimate=pl.CostEstimate(
            flops=2 * 10**10, bytes_accessed=30 * 10**6, transcendentals=2 * 10**6
        ),
        name="finish",
    )(*arrays)


def local(
    clean,
    noise,
    lowres,
    aug_noise,
    timesteps,
    aug_levels,
    lengths,
    text,
    w_stem,
    w_time,
    conv_one,
    conv_two,
    kv_weight,
    w_query,
    w_output,
    w_head,
):
    images = clean.shape[0]
    tokens = text.shape[1]
    features = text.shape[2]
    width = kv_weight.shape[1]
    half = kv_weight.shape[0]
    bf16, f32 = jnp.bfloat16, jnp.float32
    far = lax.ppermute(kv_weight, "mp", [(0, 1), (1, 0)])

    step, level = timesteps[:, None], aug_levels[:, None]
    which = np.arange(4)
    signal = signal_level(jnp.where(which < 2, step, level))
    coefs = jnp.sqrt(jnp.where(which % 2 == 0, signal, 1.0 - signal))
    lane = np.arange(4 * FREQS)
    freqs = jnp.exp(-math.log(10000.0) * (lane % FREQS).astype(np.float32) / FREQS)
    angles = jnp.where(lane < 2 * FREQS, step, level).astype(f32) * freqs
    feature = jnp.where(lane % (2 * FREQS) < FREQS, jnp.sin(angles), jnp.cos(angles))
    clean, noise, lowres, aug_noise = (
        jnp.transpose(a, (1, 0, 2)) for a in (clean, noise, lowres, aug_noise)
    )
    made = forward(
        coefs, feature, clean, noise, lowres, aug_noise, w_stem, w_time, conv_one, conv_two
    )
    mp = lax.axis_index("mp").astype(jnp.int32).reshape(1)
    flat_text = text.reshape(images * tokens, features)
    mid, out, wide_one, wide_two, stats = made
    cot, wide_grad, loss = attention(
        mp, lengths, noise, flat_text, kv_weight, far, mid, stats, w_query, w_output, w_head
    )
    counts = (
        2 * half * width,
        conv_one.shape[0] * conv_one.shape[1],
        images * lax.axis_size(DP_MP) * clean.shape[0] * clean.shape[2],
    )
    conv_one_update, conv_two_update, kv, mean = finish(
        counts, flat_text, cot, loss, out, wide_one, wide_two, wide_grad, stats, conv_two
    )
    return (conv_one_update, conv_two_update, kv.T, mean[0, 0])


def solution(mesh):
    finer = Mesh(
        mesh.devices.reshape(2, 4, 4, 2, mesh.shape["mp"]), ("dp_0", "dp_1", "dp_2", "dp_3", "mp")
    )
    placed = (
        P(DP_MP, None, None),
        P(DP_MP, None, None),
        P(DP_MP, None, None),
        P(DP_MP, None, None),
        P(DP_MP),
        P(DP_MP),
        P(DP_MP),
        P(DP_MP, None, None),
        P(),
        P(),
        P(),
        P(),
        P("mp", None),
        P(),
        P(),
        P(),
    )
    return jax.shard_map(
        local,
        mesh=finer,
        in_specs=placed,
        out_specs=(P(DP_MP, None), P(DP_MP, None), P("mp", DP), P()),
        check_vma=False,
    )
```

time: 141 us -> 113 us (0.80)
  Pallas kernels: 126 us -> 98 us
    pallas_call x1, Pallas kernels: 57.4 us -> 22 us  [attention(): pl.pallas_call(attend_kernel, out_shape=(jax.ShapeDtypeStruct((2 * C, ima...]
    pallas_call x1, Pallas kernels: 38.8 us -> 52.9 us  [finish(): pl.pallas_call(functools.partial(finish_kernel, counts), out_shape=(jax.S...]
    pallas_call x1, Pallas kernels: 29.8 us -> 23.1 us  [forward(): pl.pallas_call(forward_kernel, out_shape=(flat, flat, wide, wide, jax.Sha...]
where the time goes in v3:
time: 113 us
  Pallas kernels  98 us (87%)
  local copies, waits for them, and re-layouts  8.98 us (8%)
  starting transfers between devices  2.11 us (2%)
  between operations  1.95 us (2%)
  other arithmetic  1.67 us (1%)
    pallas_call x1, Pallas kernels, finish(): pl.pallas_call(functools.partial(finish_kernel, counts), out_shape=(jax.S...  52.9 us
    pallas_call x1, Pallas kernels, forward(): pl.pallas_call(forward_kernel, out_shape=(flat, flat, wide, wide, jax.Sha...  23.1 us
    pallas_call x1, Pallas kernels, attention(): pl.pallas_call(attend_kernel, out_shape=(jax.ShapeDtypeStruct((2 * C, ima...  22 us
    unnamed x35, local copies, waits for them, and re-layouts  8.98 us
  transfers between devices with their start and end apart: 1, of which 0 were waited for; matrix products, arithmetic and copies ran while one was open for 1% of the time, Pallas kernels for 21%

profile of v3, /device:TPU:0, one launch (start us, length us, event | category | flops | bytes accessed | tf_op | source)
XLA Modules:
  0.0 112.7 jit_solution(5901546116193652596)
XLA Ops:
  0.6 2.1 %collective-permute-start = (bf16[2048,256]{1,0:T(8,128)(2,1)}, bf16[2048,256]{1,0:T(8,128)(2,1)S(1)}, u32[]{:S(2)}, u32[]{:S(2)}) collective-permute-start(bf16[2048,256]{1,0:T(8,128)(2,1)} %near_ref.1), channel_id=1, source_target_pairs={{0,1},{1,0},{2,3},{3,2},{4,5},{5,4},{6,7},{7,6},{8,9},{9,8},{10,11... | collective-permute-start | bytes 3145736 | tf_op jit(solution)/shard_map/ppermute | solution.py:874
  2.7 0.8 cosine_select_fusion.feature_ref
  3.6 0.8 fusion.coef_ref
  4.4 0.0 copy-start.2
  4.4 1.0 copy-done.2
  5.4 0.0 copy-start.3
  5.4 1.0 copy-done.3
  6.4 0.0 copy-start.5
  6.4 0.9 copy-done.5
  7.3 0.0 copy-start.6
  7.3 0.9 copy-done.6
  8.2 0.0 copy-start.7
  8.2 0.9 copy-done.7
  9.1 0.0 copy-start.8
  9.1 0.9 copy-done.8
  10.0 0.0 copy-start.9
  10.0 0.9 copy-done.9
  10.9 0.0 copy-start.13
  10.9 0.7 copy-done.13
  11.6 0.0 copy-start
  11.6 0.0 copy-start.1
  11.6 0.0 copy-start.10
  11.6 0.0 copy-start.11
  11.6 0.0 copy-start.12
  11.6 0.0 copy-start.14
  11.6 0.0 copy-start.15
  11.6 23.1 %forward.1 = (f32[2,4096,128]{2,1,0:T(8,128)S(1)}, f32[2,4096,128]{2,1,0:T(8,128)S(1)}, bf16[2,66,64,384]{3,2,1,0:T(8,128)(2,1)S(1)}, bf16[2,66,64,384]{3,2,1,0:T(8,128)(2,1)S(1)}, f32[2,8,128]{2,1,0:T(8,128)S(1)}) custom-call(f32[2,4]{1,0:T(2,128)S(1)} %fusion.coef_ref, f32[2,256]{1,0:T(2,128)S(1)} %cosine_select_fusion.feature_ref, ...), custom_call_target="tpu_custom_call" | custom-call | flops 10000000000 | bytes 22000000 | tf_op jit(solution)/shard_map/forward/pallas_call | solution.py:266
  34.8 0.0 collective-permute-done.far_ref
  34.8 0.0 copy-done
  34.8 0.0 copy-done.1
  34.8 0.0 copy-done.10
  34.8 0.0 copy-done.11
  34.8 0.0 copy-done.12
  34.8 0.0 copy-done.14
  34.8 0.0 copy-done.15
  34.8 0.0 copy-start.4
  34.9 22.0 %attention.1 = (bf16[256,256]{1,0:T(8,128)(2,1)S(1)}, bf16[2,66,64,384]{3,2,1,0:T(8,128)(2,1)S(1)}, f32[1,128]{1,0:T(1,128)S(1)}) custom-call(s32[1]{0:T(128)} %bitcast.1.half_ref, s32[2]{0:T(128)S(1)} %copy-done.15, f32[3,2,4096]{2,1,0:T(2,128)S(1)} %bitcast.16, bf16[256,4096]{1,0:T(8,128)(2,1)S(1)} %bitcast.10, bf16[2048,256]{1,0:T(8,128)(2,1)S(1)} %copy-done.1, ...), custom_call_target="tpu_custom_call" | custom-call | flops 10000000000 | bytes 16000000 | tf_op jit(solution)/shard_map/attention/pallas_call | solution.py:430
  56.8 0.0 copy-done.4
  56.8 52.9 %finish.1 = (f32[9,128]{1,0:T(8,128)S(1)}, f32[9,128]{1,0:T(8,128)S(1)}, f32[4,2048]{1,0:T(4,128)S(1)}, f32[1,128]{1,0:T(1,128)S(1)}) custom-call(bf16[256,4096]{1,0:T(8,128)(2,1)S(1)} %bitcast.11, bf16[256,256]{1,0:T(8,128)(2,1)S(1)} %get-tuple-element.18.cot_ref, f32[1,128]{1,0:T(1,128)S(1)} %get-tuple-element.19.loss_ref, ...), custom_call_target="tpu_custom_call" | custom-call | flops 20000000000 | bytes 30000000 | tf_op jit(solution)/shard_map/finish/pallas_call | solution.py:814
  109.7 0.6 copy.29
  110.3 0.6 copy.30
  110.9 0.6 copy.31
Async XLA Ops:
  0.6 34.1 %collective-permute-start = (bf16[2048,256]{1,0:T(8,128)(2,1)}, bf16[2048,256]{1,0:T(8,128)(2,1)S(1)}, u32[]{:S(2)}, u32[]{:S(2)}) collective-permute-start(bf16[2048,256]{1,0:T(8,128)(2,1)} %near_ref.1), channel_id=1, source_target_pairs={{0,1},{1,0},{2,3},{3,2},{4,5},{5,4},{6,7},{7,6},{8,9},{9,8},{10,11... | collective-permute-start | bytes 3145736 | tf_op jit(solution)/shard_map/ppermute | solution.py:874
  4.4 1.0 copy-start.2
  5.4 1.0 copy-start.3
  6.4 0.9 copy-start.5
  7.3 0.9 copy-start.6
  8.2 0.9 copy-start.7
  9.1 0.9 copy-start.8
  10.0 0.9 copy-start.9
  10.9 0.7 copy-start.13
  11.6 23.2 %copy-start = (bf16[2,128,4096]{2,1,0:T(8,128)(2,1)S(1)}, bf16[2,128,4096]{2,1,0:T(8,128)(2,1)}, u32[]{:S(2)}) copy-start(bf16[2,128,4096]{2,1,0:T(8,128)(2,1)} %param.28) | copy-start | bytes 6291460
  11.6 23.2 %copy-start.1 = (bf16[2048,256]{1,0:T(8,128)(2,1)S(1)}, bf16[2048,256]{1,0:T(8,128)(2,1)}, u32[]{:S(2)}) copy-start(bf16[2048,256]{1,0:T(8,128)(2,1)} %near_ref.1) | copy-start | bytes 3145732
  11.6 23.2 %copy-start.10 = (f32[2,3,4096]{2,0,1:T(2,128)S(1)}, f32[2,3,4096]{2,0,1:T(2,128)}, u32[]{:S(2)}) copy-start(f32[2,3,4096]{2,0,1:T(2,128)} %param.22) | copy-start | bytes 294916
  11.6 23.2 %copy-start.11 = (bf16[128,128]{1,0:T(8,128)(2,1)S(1)}, bf16[128,128]{1,0:T(8,128)(2,1)}, u32[]{:S(2)}) copy-start(bf16[128,128]{1,0:T(8,128)(2,1)} %query_ref.1) | copy-start | bytes 98308
  11.6 23.2 %copy-start.12 = (bf16[128,128]{1,0:T(8,128)(2,1)S(1)}, bf16[128,128]{1,0:T(8,128)(2,1)}, u32[]{:S(2)}) copy-start(bf16[128,128]{1,0:T(8,128)(2,1)} %output_ref.1) | copy-start | bytes 98308
  11.6 23.2 %copy-start.14 = (bf16[3,128]{1,0:T(4,128)(2,1)S(1)}, bf16[3,128]{1,0:T(4,128)(2,1)}, u32[]{:S(2)}) copy-start(bf16[3,128]{1,0:T(4,128)(2,1)} %heads_ref.1) | copy-start | bytes 2308
  11.6 23.2 %copy-start.15 = (s32[2]{0:T(128)S(1)}, s32[2]{0:T(128)}, u32[]{:S(2)}) copy-start(s32[2]{0:T(128)} %lengths_ref.1) | copy-start | bytes 28
  34.8 22.0 %copy-start.4 = (bf16[1152,128]{1,0:T(8,128)(2,1)S(1)}, bf16[1152,128]{1,0:T(8,128)(2,1)}, u32[]{:S(2)}) copy-start(bf16[1152,128]{1,0:T(8,128)(2,1)} %two_ref.1) | copy-start | bytes 884740

commit v4 on v3

--- a/solution.py
+++ b/solution.py
@@ -20,14 +20,8 @@
 DP = ("dp_0", "dp_1", "dp_2", "dp_3")
 
 
-def signal_level(index):
-    ratio = (index.astype(jnp.float32) / STEPS + 0.008) / 1.008
-    cosine = jnp.cos(ratio * (math.pi / 2.0))
-    return cosine * cosine
-
-
 PIXELS = S * S
-CHUNK = 512
+CHUNK = 2048
 CHUNKS = PIXELS // CHUNK
 EDGE = S
 C = 128
@@ -122,7 +116,6 @@
 
 
 def forward_kernel(
-    coef_ref,
     feature_ref,
     clean_in,
     noise_in,
@@ -171,7 +164,7 @@
     w3 = w - w1 - w2
     stems_ref[...] = jnp.concatenate([w1, w2, w1, w3, w2, w1], axis=0).astype(jnp.bfloat16)
     feature = jnp.concatenate(
-        [feature_ref[...], jnp.zeros((8 - images, 2 * C), jnp.float32)], axis=0
+        [feature_ref[:, : 2 * C], jnp.zeros((8 - images, 2 * C), jnp.float32)], axis=0
     )
     embed = jnp.dot(
         feature,
@@ -183,13 +176,14 @@
     planes_ref[...] = jnp.zeros(planes_ref.shape, jnp.float32)
 
     def image(i, carry):
+        coefs = [row_of(feature_ref[:, 2 * C + k : 2 * C + k + 1], i) for k in range(4)]
         for k in range(3):
             planes_ref[k : k + 1] = (
-                coef_ref[i, 0] * row_of(clean_ref[k], i)
-                + coef_ref[i, 1] * row_of(noise_ref[k], i)
+                coefs[0] * row_of(clean_ref[k], i)
+                + coefs[1] * row_of(noise_ref[k], i)
             )
             planes_ref[3 + k : 4 + k] = (
-                coef_ref[i, 2] * row_of(low_ref[k], i) + coef_ref[i, 3] * row_of(aug_ref[k], i)
+                coefs[2] * row_of(low_ref[k], i) + coefs[3] * row_of(aug_ref[k], i)
             )
         s = planes_ref[...]
         s1 = s.astype(jnp.bfloat16).astype(jnp.float32)
@@ -258,7 +252,7 @@
     lax.fori_loop(0, images, image, 0)
 
 
-def forward(coefs, feature, *arrays):
+def forward(feature, *arrays):
     images = feature.shape[0]
     bf16, f32 = jnp.bfloat16, jnp.float32
     wide = jax.ShapeDtypeStruct((images, S + 2, S, 3 * C), bf16)
@@ -266,10 +260,7 @@
     return pl.pallas_call(
         forward_kernel,
         out_shape=(flat, flat, wide, wide, jax.ShapeDtypeStruct((images, 8, C), f32)),
-        in_specs=[
-            pl.BlockSpec(memory_space=pltpu.SMEM),
-            pl.BlockSpec(memory_space=pltpu.VMEM),
-        ]
+        in_specs=[pl.BlockSpec(memory_space=pltpu.VMEM)]
         + [pl.BlockSpec(memory_space=pltpu.HBM)] * 8,
         out_specs=[pl.BlockSpec(memory_space=pltpu.VMEM)] * 5,
         scratch_shapes=[pltpu.VMEM(a.shape, a.dtype) for a in arrays]
@@ -287,7 +278,7 @@
             flops=10**10, bytes_accessed=22 * 10**6, transcendentals=2 * 10**6
         ),
         name="forward",
-    )(coefs, feature, *arrays)
+    )(feature, *(pltpu.with_memory_space_constraint(a, pltpu.HBM) for a in arrays))
 
 
 TN = (((0,), (0,)), ((), ()))
@@ -455,9 +446,9 @@
     )(half, lengths, noise, text, near, far, mid, stats, w_query, w_output, head)
 
 
-ATTEND = 1024
+ATTEND = 4096
 LIMIT_F = 12
-LIMIT_A = 16
+LIMIT_A = 20
 LIMIT_T = 20
 
 
@@ -720,9 +711,10 @@
         lax.fori_loop(0, CHUNKS, early, 0)
         weights(0, i, wide_one, lambda at: grad_pad[0, at])
 
-    for i in range(images):
+    weights(1, 0, wide_two, lambda at: wide_grad[0, at, :, C : 2 * C])
+    copies = [to_first(0, first_kv[0]), to_first(1, first_kv[1])]
+    for i in range(1, images):
         weights(1, i, wide_two, lambda at, i=i: wide_grad[i, at, :, C : 2 * C])
-    copies = [to_first(0, first_kv[0]), to_first(1, first_kv[1])]
     pack(1, 2)
     copies.append(start_core(2))
     lines = act_grad(0)
@@ -874,18 +866,24 @@
     far = lax.ppermute(kv_weight, "mp", [(0, 1), (1, 0)])
 
     step, level = timesteps[:, None], aug_levels[:, None]
-    which = np.arange(4)
-    signal = signal_level(jnp.where(which < 2, step, level))
-    coefs = jnp.sqrt(jnp.where(which % 2 == 0, signal, 1.0 - signal))
-    lane = np.arange(4 * FREQS)
+    width_f = 4 * FREQS
+    lane = np.arange(width_f + C)
+    coef = lane >= width_f
+    on_step = np.where(coef, (lane - width_f) < 2, lane < 2 * FREQS)
+    index = jnp.where(on_step, step, level).astype(f32)
     freqs = jnp.exp(-math.log(10000.0) * (lane % FREQS).astype(np.float32) / FREQS)
-    angles = jnp.where(lane < 2 * FREQS, step, level).astype(f32) * freqs
-    feature = jnp.where(lane % (2 * FREQS) < FREQS, jnp.sin(angles), jnp.cos(angles))
+    ratio = (index / STEPS + 0.008) / 1.008
+    angles = jnp.where(coef, ratio * (math.pi / 2.0), index * freqs)
+    cosine = jnp.cos(angles)
+    signal = cosine * cosine
+    signal = jnp.sqrt(jnp.where(lane % 2 == 0, signal, 1.0 - signal))
+    wave = jnp.where(lane % (2 * FREQS) < FREQS, jnp.sin(angles), cosine)
+    feature = jnp.where(coef, signal, wave)
     clean, noise, lowres, aug_noise = (
         jnp.transpose(a, (1, 0, 2)) for a in (clean, noise, lowres, aug_noise)
     )
     made = forward(
-        coefs, feature, clean, noise, lowres, aug_noise, w_stem, w_time, conv_one, conv_two
+        feature, clean, noise, lowres, aug_noise, w_stem, w_time, conv_one, conv_two
     )
     mp = lax.axis_index("mp").astype(jnp.int32).reshape(1)
     flat_text = text.reshape(images * tokens, features)

time: 113 us -> 95.9 us (0.85)
  Pallas kernels: 98 us -> 86.1 us
  local copies, waits for them, and re-layouts: 8.98 us -> 4.58 us
    pallas_call x1, Pallas kernels: 22 us -> 16.3 us  [attention(): pl.pallas_call(attend_kernel, out_shape=(jax.ShapeDtypeStruct((2 * C, ima...]
    unnamed x35 -> x23, local copies, waits for them, and re-layouts: 8.98 us -> 4.58 us
    pallas_call x1, Pallas kernels: 52.9 us -> 49.1 us  [finish(): pl.pallas_call(functools.partial(finish_kernel, counts), out_shape=(jax.S...]
    pallas_call x1, Pallas kernels: 23.1 us -> 20.7 us  [forward(): pl.pallas_call(forward_kernel, out_shape=(flat, flat, wide, wide, jax.Sha...]
  transfers between devices with their start and end apart: 1 -> 1, of which waited for: 0 -> 0; matrix products, arithmetic and copies ran while one was open for 1% -> 1% of each run, Pallas kernels for 21% -> 22%
where the time goes in v4:
time: 95.9 us; the launch traced here: 95.7 us
  Pallas kernels  86.1 us (90%)
  local copies, waits for them, and re-layouts  4.58 us (5%)
  starting transfers between devices  2.11 us (2%)
  between operations  1.95 us (2%)
    pallas_call x1, Pallas kernels, finish(): pl.pallas_call(functools.partial(finish_kernel, counts), out_shape=(jax.S...  49.1 us
    pallas_call x1, Pallas kernels, forward(): pl.pallas_call(forward_kernel, out_shape=(flat, flat, wide, wide, jax.Sha...  20.7 us
    pallas_call x1, Pallas kernels, attention(): pl.pallas_call(attend_kernel, out_shape=(jax.ShapeDtypeStruct((2 * C, ima...  16.3 us
    unnamed x23, local copies, waits for them, and re-layouts  4.58 us
    ppermute x1, starting transfers between devices, local(): far = lax.ppermute(kv_weight, 'mp', [(0, 1), (1, 0)])  2.11 us
  transfers between devices with their start and end apart: 1, of which 0 were waited for; matrix products, arithmetic and copies ran while one was open for 1% of the time, Pallas kernels for 22%

profile of v4, /device:TPU:0, one launch (start us, length us, event | category | flops | bytes accessed | tf_op | source)
XLA Modules:
  0.0 95.7 jit_solution(10256107583441460000)
XLA Ops:
  0.6 2.1 %collective-permute-start = (bf16[2048,256]{1,0:T(8,128)(2,1)}, bf16[2048,256]{1,0:T(8,128)(2,1)S(1)}, u32[]{:S(2)}, u32[]{:S(2)}) collective-permute-start(bf16[2048,256]{1,0:T(8,128)(2,1)} %near_ref.1), channel_id=1, source_target_pairs={{0,1},{1,0},{2,3},{3,2},{4,5},{5,4},{6,7},{7,6},{8,9},{9,8},{10,11... | collective-permute-start | bytes 3145736 | tf_op jit(solution)/shard_map/ppermute | solution.py:866
  2.7 0.9 fusion.1.feature_ref
  3.7 0.0 copy-start
  3.7 0.0 copy-start.1
  3.7 0.0 copy-start.3
  3.7 0.0 copy-start.4
  3.7 0.0 copy-start.5
  3.7 0.0 copy-start.6
  3.7 0.0 copy-start.7
  3.7 20.7 %forward.1 = (f32[2,4096,128]{2,1,0:T(8,128)S(1)}, f32[2,4096,128]{2,1,0:T(8,128)S(1)}, bf16[2,66,64,384]{3,2,1,0:T(8,128)(2,1)S(1)}, bf16[2,66,64,384]{3,2,1,0:T(8,128)(2,1)S(1)}, f32[2,8,128]{2,1,0:T(8,128)S(1)}) custom-call(f32[2,384]{1,0:T(2,128)S(1)} %fusion.1.feature_ref, f32[3,2,4096]{2,1,0:T(2,128)} %bitcast.15, f32[3,2,4096]{2,1,0:T(2,128)} %bitcast.12, ...), custom_call_target="tpu_custom_call" | custom-call | flops 10000000000 | bytes 22000000 | tf_op jit(solution)/shard_map/forward/pallas_call | solution.py:260
  24.5 0.0 copy-start.8
  24.5 2.7 %copy-done.8 = bf16[2,66,64,384]{3,2,1,0:T(8,128)(2,1)} copy-done((bf16[2,66,64,384]{3,2,1,0:T(8,128)(2,1)}, bf16[2,66,64,384]{3,2,1,0:T(8,128)(2,1)S(1)}, u32[]{:S(2)}) %copy-start.8) | copy-done | bytes 6488088
  27.2 0.0 collective-permute-done.far_ref
  27.2 0.0 copy-done
  27.2 0.0 copy-done.1
  27.2 0.0 copy-done.3
  27.2 0.0 copy-done.4
  27.2 0.0 copy-done.5
  27.2 0.0 copy-done.6
  27.2 0.0 copy-done.7
  27.2 0.0 copy-start.2
  27.3 0.0 copy-start.9
  27.3 16.3 %attention.1 = (bf16[256,256]{1,0:T(8,128)(2,1)S(1)}, bf16[2,66,64,384]{3,2,1,0:T(8,128)(2,1)S(1)}, f32[1,128]{1,0:T(1,128)S(1)}) custom-call(s32[1]{0:T(128)} %bitcast.1.half_ref, s32[2]{0:T(128)S(1)} %copy-done.7, f32[3,2,4096]{2,1,0:T(2,128)S(1)} %bitcast.13, bf16[256,4096]{1,0:T(8,128)(2,1)S(1)} %bitcast.10, bf16[2048,256]{1,0:T(8,128)(2,1)S(1)} %copy-done.1, ...), custom_call_target="tpu_custom_call" | custom-call | flops 10000000000 | bytes 16000000 | tf_op jit(solution)/shard_map/attention/pallas_call | solution.py:421
  43.6 0.0 copy-done.2
  43.6 0.0 copy-done.9
  43.6 49.1 %finish.1 = (f32[9,128]{1,0:T(8,128)S(1)}, f32[9,128]{1,0:T(8,128)S(1)}, f32[4,2048]{1,0:T(4,128)S(1)}, f32[1,128]{1,0:T(1,128)S(1)}) custom-call(bf16[256,4096]{1,0:T(8,128)(2,1)S(1)} %bitcast.11, bf16[256,256]{1,0:T(8,128)(2,1)S(1)} %get-tuple-element.18.cot_ref, f32[1,128]{1,0:T(1,128)S(1)} %get-tuple-element.19.loss_ref, ...), custom_call_target="tpu_custom_call" | custom-call | flops 20000000000 | bytes 30000000 | tf_op jit(solution)/shard_map/finish/pallas_call | solution.py:806
  92.7 0.6 copy.29
  93.3 0.6 copy.30
  93.9 0.6 copy.31
Async XLA Ops:
  0.6 26.6 %collective-permute-start = (bf16[2048,256]{1,0:T(8,128)(2,1)}, bf16[2048,256]{1,0:T(8,128)(2,1)S(1)}, u32[]{:S(2)}, u32[]{:S(2)}) collective-permute-start(bf16[2048,256]{1,0:T(8,128)(2,1)} %near_ref.1), channel_id=1, source_target_pairs={{0,1},{1,0},{2,3},{3,2},{4,5},{5,4},{6,7},{7,6},{8,9},{9,8},{10,11... | collective-permute-start | bytes 3145736 | tf_op jit(solution)/shard_map/ppermute | solution.py:866
  3.7 23.5 %copy-start = (bf16[2,128,4096]{2,1,0:T(8,128)(2,1)S(1)}, bf16[2,128,4096]{2,1,0:T(8,128)(2,1)}, u32[]{:S(2)}) copy-start(bf16[2,128,4096]{2,1,0:T(8,128)(2,1)} %param.28) | copy-start | bytes 6291460
  3.7 23.5 %copy-start.1 = (bf16[2048,256]{1,0:T(8,128)(2,1)S(1)}, bf16[2048,256]{1,0:T(8,128)(2,1)}, u32[]{:S(2)}) copy-start(bf16[2048,256]{1,0:T(8,128)(2,1)} %near_ref.1) | copy-start | bytes 3145732
  3.7 23.5 %copy-start.3 = (f32[2,3,4096]{2,0,1:T(2,128)S(1)}, f32[2,3,4096]{2,0,1:T(2,128)}, u32[]{:S(2)}) copy-start(f32[2,3,4096]{2,0,1:T(2,128)} %param.22) | copy-start | bytes 294916
  3.7 23.5 %copy-start.4 = (bf16[128,128]{1,0:T(8,128)(2,1)S(1)}, bf16[128,128]{1,0:T(8,128)(2,1)}, u32[]{:S(2)}) copy-start(bf16[128,128]{1,0:T(8,128)(2,1)} %query_ref.1) | copy-start | bytes 98308
  3.7 23.5 %copy-start.5 = (bf16[128,128]{1,0:T(8,128)(2,1)S(1)}, bf16[128,128]{1,0:T(8,128)(2,1)}, u32[]{:S(2)}) copy-start(bf16[128,128]{1,0:T(8,128)(2,1)} %output_ref.1) | copy-start | bytes 98308
  3.7 23.5 %copy-start.6 = (bf16[3,128]{1,0:T(4,128)(2,1)S(1)}, bf16[3,128]{1,0:T(4,128)(2,1)}, u32[]{:S(2)}) copy-start(bf16[3,128]{1,0:T(4,128)(2,1)} %heads_ref.1) | copy-start | bytes 2308
  3.7 23.5 %copy-start.7 = (s32[2]{0:T(128)S(1)}, s32[2]{0:T(128)}, u32[]{:S(2)}) copy-start(s32[2]{0:T(128)} %lengths_ref.1) | copy-start | bytes 28
  24.5 2.7 %copy-start.8 = (bf16[2,66,64,384]{3,2,1,0:T(8,128)(2,1)}, bf16[2,66,64,384]{3,2,1,0:T(8,128)(2,1)S(1)}, u32[]{:S(2)}) copy-start(bf16[2,66,64,384]{3,2,1,0:T(8,128)(2,1)S(1)} %get-tuple-element.22.wide_two) | copy-start | bytes 19464196
  27.2 16.3 %copy-start.2 = (bf16[1152,128]{1,0:T(8,128)(2,1)S(1)}, bf16[1152,128]{1,0:T(8,128)(2,1)}, u32[]{:S(2)}) copy-start(bf16[1152,128]{1,0:T(8,128)(2,1)} %two_ref.1) | copy-start | bytes 884740
  27.3 16.3 %copy-start.9 = (bf16[2,66,64,384]{3,2,1,0:T(8,128)(2,1)S(1)}, bf16[2,66,64,384]{3,2,1,0:T(8,128)(2,1)}, u32[]{:S(2)}) copy-start(bf16[2,66,64,384]{3,2,1,0:T(8,128)(2,1)} %copy-done.8) | copy-start | bytes 19464196
